TPU v7x, 32 devices: a whole 2x2x4 slice. The times are simulated.
32 devices in a mesh: batch: 8 (over z, x), cols: 4 (over y, core).
Axes of the slice: x: 2, y: 2, z: 4, core: 2. Of those that a mesh axis runs over, the one named last changes fastest.
Arguments:
- partial_query: float32 [8, 1024, 1024], P('batch', None, 'cols'), may hold values from -0.875 to 0.875
- partial_key: float32 [8, 1024, 1024], P('batch', None, 'cols'), may hold values from -0.875 to 0.875
- partial_value: float32 [8, 1024, 1024], P('batch', None, 'cols'), may hold values from -0.875 to 0.875
- partial_mixed: float32 [8, 1024, 1024], P('batch', 'cols'), may hold values from -0.875 to 0.875
- partial_norm: float32 [8, 1024], P('batch'), may hold values from -8 to 8
- partial_bias: float32 [8, 1024], P('batch'), may hold values from -8 to 8
- master_query: float32 [1024, 1024], P('batch', 'cols'), may hold values from -0.1875 to 0.1875
- master_key: float32 [1024, 1024], P('batch', 'cols'), may hold values from -0.1875 to 0.1875
- master_value: float32 [1024, 1024], P('batch', 'cols'), may hold values from -0.1875 to 0.1875
- master_mixed: float32 [1024, 1024], P('cols', 'batch'), may hold values from -0.1875 to 0.1875
- master_norm: float32 [1024], P('batch'), may hold values from 0.25 to 1.75
- master_bias: float32 [1024], P('batch'), may hold values from -3 to 3
Outputs:
- compute_query: bfloat16 [1024, 1024], P(None, 'cols')
- compute_key: bfloat16 [1024, 1024], P(None, 'cols')
- compute_value: bfloat16 [1024, 1024], P(None, 'cols')
- compute_mixed: bfloat16 [1024, 1024], P('cols')
- compute_norm: bfloat16 [1024], replicated
- compute_bias: bfloat16 [1024], replicated
- stepped_query: float32 [1024, 1024], P('batch', 'cols')
- stepped_key: float32 [1024, 1024], P('batch', 'cols')
- stepped_value: float32 [1024, 1024], P('batch', 'cols')
- stepped_mixed: float32 [1024, 1024], P('cols', 'batch')
- stepped_norm: float32 [1024], P('batch')
- stepped_bias: float32 [1024], P('batch')
All inputs are finite; a program needn't handle non-finite values.
Results may differ from a plain program's by a relative error of at most 0.001.
Values may be sent and summed in bfloat16 or wider, within the bound.
No kernel may reach another device: no remote copies, remote signals or barrier semaphores. Data moves between devices by JAX's collectives and lax.ppermute only.
A program may use at most 64 MiB of HBM per device.

v0:
```python
import math

import jax
import jax.numpy as jnp
from jax import lax
from jax.experimental import pallas as pl
from jax.experimental.pallas import tpu as pltpu
from jax.sharding import PartitionSpec as P


learn_rate = 0.4
lanes = 128
tail_rows = 16
vmem_grant = 16 << 20
largest_partial = 12.0


def sizes_of(query, mixed, replicas):
    rows, cols = query.shape[0] // replicas, query.shape[1]
    fits = (
        rows % lanes == 0
        and cols == 2 * rows
        and mixed.shape == (cols, rows * replicas)
    )
    return rows, cols, fits


def groups_of(fits):
    return [(0, 1), (2, 3, 4, 5)] if fits else [(0, 1, 2, 3, 4, 5)]


def split(x):
    wide = x * 8193.0
    high = wide - (wide - x)
    return high, x - high


def own_lines(line, here, height):
    high, low = split(line)
    row = lax.broadcasted_iota(jnp.int32, (height, line.shape[-1]), 0)
    return jnp.where(row == 2 * here, high, 0.0) + jnp.where(row == 2 * here + 1, low, 0.0)


def pack_plain(arrays, chunks, replicas, here):
    query, key, value, mixed, norm, bias = arrays
    rows, cols, _ = sizes_of(query, mixed, replicas)
    out = []
    for at in chunks:
        parts = [lax.dynamic_slice_in_dim(a, at * rows, rows, 0) for a in (query, key, value)]
        parts.append(lax.dynamic_slice_in_dim(mixed, at * rows, rows, 1).reshape(rows, cols))
        pair = [lax.dynamic_slice_in_dim(a, at * rows, rows, 0) for a in (norm, bias)]
        line = jnp.pad(jnp.concatenate(pair), (0, cols - 2 * rows))[None]
        if here is not None:
            line = own_lines(line, here, 2 * replicas)
        out.append(jnp.concatenate(parts + [line]))
    return out


def pack_tiles(arrays, offsets, replicas):
    query, key, value, mixed, norm, bias = arrays
    rows, cols, _ = sizes_of(query, mixed, replicas)
    height = 4 * rows + 2 * replicas

    def kernel(q, k, v, m, n, b, out, lines, sems, line_sem):
        here = lax.axis_index("batch")
        vectors = [pltpu.make_async_copy(ref, lines.at[pl.ds(i, 1)], line_sem.at[0]) for i, ref in enumerate((n, b))]
        for c in vectors:
            c.start()
        started = []
        for j, offset in enumerate(offsets):
            start = pl.multiple_of((here ^ offset) * rows, lanes)
            copies = []
            for i, ref in enumerate((q, k, v)):
                copies.append((ref.at[pl.ds(start, rows), :], out.at[j, pl.ds(i * rows, rows), :]))
            for i in range(2):
                copies.append(
                    (
                        m.at[pl.ds(i * rows, rows), pl.ds(start, rows)],
                        out.at[j, pl.ds(3 * rows, rows), pl.ds(i * rows, rows)],
                    )
                )
            started += [pltpu.make_async_copy(*c, sems.at[j]) for c in copies]
        for c in started:
            c.start()
        for c in vectors:
            c.wait()
        for j, offset in enumerate(offsets):
            start = pl.multiple_of((here ^ offset) * rows, lanes)
            for i in range(2):
                own = own_lines(lines[pl.ds(i, 1), pl.ds(start, rows)], here, 2 * replicas)
                out[j, pl.ds(4 * rows, 2 * replicas), pl.ds(i * rows, rows)] = own
        for c in started:
            c.wait()

    partials = (query, key, value, mixed, norm[None], bias[None])
    slabs = pl.pallas_call(
        kernel,
        out_shape=jax.ShapeDtypeStruct((len(offsets), height, cols), jnp.float32),
        in_specs=[pl.BlockSpec(memory_space=pltpu.HBM)] * 6,
        out_specs=pl.BlockSpec(memory_space=pltpu.VMEM),
        scratch_shapes=[
            pltpu.VMEM((2, rows * replicas), jnp.float32),
            pltpu.SemaphoreType.DMA((len(offsets),)),
            pltpu.SemaphoreType.DMA((1,)),
        ],
        compiler_params=pltpu.CompilerParams(vmem_limit_bytes=vmem_grant),
    )(*[pltpu.with_memory_space_constraint(x, pltpu.HBM) for x in partials])
    return [slabs[j] for j in range(len(offsets))]


def step_plain(total, masters, parts, rate, rows, cols):
    own = [masters[i] - rate * total[i * rows : (i + 1) * rows] for i in range(3)]
    own.append(masters[3] - rate * total[3 * rows : 4 * rows].reshape(cols, rows))
    line = jnp.sum(total[4 * rows :], axis=0)
    own += [masters[4] - rate * line[:rows], masters[5] - rate * line[rows : 2 * rows]]
    line = jnp.pad(jnp.concatenate(own[4:]), (0, cols - 2 * rows))[None]
    slab = own[:3] + [own[3].reshape(rows, cols), jnp.broadcast_to(line, (tail_rows, cols))]
    return jnp.concatenate([x.astype(jnp.bfloat16) for x in slab]), own


def step_tiles(total, masters, parts, rate, rows, cols):
    masters = [masters[p] if p < 4 else masters[p][None] for p in parts]
    height = rows * sum(p < 4 for p in parts)
    tail = tail_rows if 4 in parts else 0

    def kernel(total, *refs):
        olds, slab, news = refs[: len(parts)], refs[len(parts)], refs[len(parts) + 1 :]
        if tail:
            line = jnp.sum(total[pl.ds(height, total.shape[0] - height), :], axis=0, keepdims=True)
        for i, (p, old, new) in enumerate(zip(parts, olds, news)):
            if p < 3:
                at = pl.ds(i * rows, rows)
                new[...] = old[...] - rate * total[at, :]
                slab[at, :] = new[...].astype(jnp.bfloat16)
            elif p == 3:
                for h in range(2):
                    at, half = pl.ds(i * rows, rows), pl.ds(h * rows, rows)
                    new[half, :] = old[half, :] - rate * total[at, half]
                    slab[at, half] = new[half, :].astype(jnp.bfloat16)
            else:
                half = slice((p - 4) * rows, (p - 3) * rows)
                new[...] = old[...] - rate * line[:, half]
                ends = jnp.broadcast_to(new[...], (tail, rows)).astype(jnp.bfloat16)
                slab[pl.ds(height, tail), half] = ends

    vmem = pl.BlockSpec(memory_space=pltpu.VMEM)
    slab, *own = pl.pallas_call(
        kernel,
        out_shape=[jax.ShapeDtypeStruct((height + tail, cols), jnp.bfloat16)]
        + [jax.ShapeDtypeStruct(x.shape, jnp.float32) for x in masters],
        in_specs=[vmem] * (1 + len(parts)),
        out_specs=[vmem] * (1 + len(parts)),
        name="step",
        compiler_params=pltpu.CompilerParams(vmem_limit_bytes=vmem_grant),
    )(total, *masters)
    return slab, [x if p < 4 else x.reshape(-1) for p, x in zip(parts, own)]


def unpack_tiles(pieces, tick, parts, rows, cols):
    replicas = len(pieces)
    height = rows * sum(p < 4 for p in parts)
    vectors = [p for p in parts if p > 3]

    def kernel(*refs):
        got, outs = refs[:replicas], refs[replicas + 1 : replicas + 1 + len(parts)]
        *lines, sem = refs[replicas + 1 + len(parts) :]
        here = lax.axis_index("batch")
        started = []
        for j, piece in enumerate(got):
            start = pl.multiple_of((here ^ j) * rows, lanes)
            for i, (p, out) in enumerate(zip(parts, outs)):
                at = pl.ds(i * rows, rows)
                if p < 3:
                    pairs = [(piece.at[at, :], out.at[pl.ds(start, rows), :])]
                elif p == 3:
                    halves = [pl.ds(h * rows, rows) for h in range(2)]
                    pairs = [(piece.at[at, half], out.at[half, pl.ds(start, rows)]) for half in halves]
                else:
                    pairs = []
                started += [pltpu.make_async_copy(*pair, sem.at[0]) for pair in pairs]
        for c in started:
            c.start()
        for j, piece in enumerate(got):
            for p, line in zip(vectors, lines):
                tail = piece[pl.ds(height, tail_rows), pl.ds((p - 4) * rows, rows)]
                line[pl.ds(here ^ j, 1), :] = tail.astype(jnp.float32)[0:1]
        for line, out in zip(lines, outs[len(parts) - len(vectors) :]):
            out[...] = line[...].astype(jnp.bfloat16)
        for c in started:
            c.wait()

    shapes = [(replicas * rows, cols)] * 3 + [(cols, replicas * rows)] + [(replicas, rows)] * 2
    hbm = pl.BlockSpec(memory_space=pltpu.HBM)
    vmem = pl.BlockSpec(memory_space=pltpu.VMEM)
    outs = pl.pallas_call(
        kernel,
        out_shape=[jax.ShapeDtypeStruct(shapes[p], jnp.bfloat16) for p in parts],
        in_specs=[vmem] * (replicas + 1),
        out_specs=[hbm if p < 4 else vmem for p in parts],
        scratch_shapes=[pltpu.VMEM((replicas, rows), jnp.float32) for _ in vectors] + [pltpu.SemaphoreType.DMA((1,))],
        name="unpack",
        compiler_params=pltpu.CompilerParams(vmem_limit_bytes=vmem_grant),
    )(*pieces, tick)
    return [x if p < 4 else x.reshape(-1) for p, x in zip(parts, outs)]


def unpack_plain(pieces, rows, cols, replicas):
    here = lax.axis_index("batch")
    stacked = jnp.stack(pieces)
    ordered = stacked[jnp.arange(replicas) ^ here]
    full = [ordered[:, i * rows : (i + 1) * rows].reshape(replicas * rows, cols) for i in range(3)]
    mixed = ordered[:, 3 * rows : 4 * rows].reshape(replicas, cols, rows)
    full.append(mixed.transpose(1, 0, 2).reshape(cols, replicas * rows))
    tail = ordered[:, 4 * rows]
    return (*full, tail[:, :rows].reshape(-1), tail[:, rows : 2 * rows].reshape(-1))


order_of_8 = (
    (0, 7, 0), (0, 7, 1), (0, 5, 0), (0, 6, 1), (0, 3, 0), (0, 6, 0), (0, 5, 1), (0, 1, 0), (0, 3, 1),
    (0, 4, 0), (0, 2, 0), (0, 4, 1), (0, 2, 1), (0, 1, 1), (1, 4, 0), (1, 1, 0), (1, 2, 0), (1, 4, 1),
    (1, 1, 1), (1, 2, 1), (1, 3, 0), (1, 5, 0), (1, 5, 1), (1, 6, 0), (1, 3, 1), (1, 6, 1), (1, 7, 0),
    (1, 7, 1),
)
bits_of_8 = {(0, 7, 1): 2, (1, 7, 0): 2}
packs_of_8 = ((7,), (6, 5, 3, 1,), (4, 2, 0,))


def plan_of(replicas, fits):
    groups = groups_of(fits)
    every = [(w, j, g) for w in range(2) for j in range(1, replicas) for g in range(len(groups))]
    bits = {at: at[1] & -at[1] for at in every}
    if fits and replicas == 8:
        bits.update(bits_of_8)
        return groups, bits, list(order_of_8)
    chunks = [*range(replicas - 1, 0, -2), *range(replicas - 2, 0, -2)]
    back = sorted(range(1, replicas), key=lambda j: (j & 1, j.bit_count(), j))
    return groups, bits, [(w, j, g) for w, order in ((0, chunks), (1, back)) for j in order for g in range(len(groups))]


def inputs_of(at, bits):
    w, j, g = at
    if w == 0:
        return [k for k in bits if k[0] == 0 and k[2] == g and k[1] ^ bits[k] == j]
    if j != bits[at]:
        return [(1, j ^ bits[at], g)]
    return [k for k in bits if k[0] == 0 and k[2] == g and k[1] == bits[k]]


def ticks_of(bits, order):
    late, seen = {}, set()
    for before, at in zip(order, order[1:]):
        new = [k for k in inputs_of(at, bits) if k not in seen]
        seen.update(new)
        if new and new != [before]:
            late[before] = [k for k in new if k != before]
    return late


def replica_step(*arrays):
    partials = tuple(a[0] for a in arrays[:6])
    masters = arrays[6:]
    replicas = lax.axis_size("batch")
    here = lax.axis_index("batch")
    rows, cols, fits = sizes_of(partials[0], partials[3], replicas)
    scale = 2.0 ** math.floor(math.log2(65504.0 / (largest_partial * replicas)))
    groups, bits, order = plan_of(replicas, fits)
    every = range(replicas)
    calls = packs_of_8 if fits and replicas == 8 else (tuple(every),)

    if fits:
        slabs = {}
        for chunks in calls:
            slabs.update(zip(chunks, pack_tiles(partials, chunks, replicas)))
    else:
        slabs = dict(zip(every, pack_plain(partials, [here ^ j for j in every], replicas, here)))

    def swap(x, bit):
        return lax.ppermute(x, "batch", [(i, i ^ bit) for i in range(replicas)])

    tall = slabs[0].shape[0]
    bounds = []
    for g, parts in enumerate(groups):
        first = rows * sum(p < 4 for q in groups[:g] for p in q)
        bounds.append((first, tall if 4 in parts else first + rows * len(parts)))
    got = {(j, g): [] for j in slabs for g in range(len(groups))}
    ahead = None

    def total(j, g):
        nonlocal ahead
        low, high = bounds[g]
        mine = slabs[j][low:high] * scale
        if not got[j, g]:
            return mine
        if ahead is not None:
            got[j, g][0], ahead = lax.optimization_barrier((got[j, g][0], ahead))
        return sum((x.astype(jnp.float32) for x in got[j, g]), mine)

    rate = learn_rate * replicas**-0.5 / scale
    ticks = ticks_of(bits, order) if fits else {}
    tick = masters[4][None]
    own, full, pieces = [None] * 6, [None] * 6, {}
    for at in order:
        w, j, g = at
        bit = bits[at]
        if w == 0:
            send = total(j, g).astype(jnp.float16)
            if got[j, g]:
                ahead = send
            got[j ^ bit, g].append(swap(send, bit))
        else:
            if (0, g) not in pieces:
                ahead = total(0, g)
                step = step_tiles if fits else step_plain
                pieces[0, g], new = step(ahead, masters, groups[g], rate, rows, cols)
                for p, x in zip(groups[g], new):
                    own[p] = x
            pieces[j, g] = swap(pieces[j ^ bit, g], bit)
        if at in ticks:
            tick = lax.optimization_barrier(tick) + 1.0
    for g, parts in enumerate(groups):
        mine = [pieces[j, g] for j in range(replicas)]
        done = unpack_tiles(mine, tick, parts, rows, cols) if fits else unpack_plain(mine, rows, cols, replicas)
        for p, x in zip(parts, done):
            full[p] = x
    return (*full, *own)


def solution(mesh):
    in_specs = (
        P("batch", None, "cols"),
        P("batch", None, "cols"),
        P("batch", None, "cols"),
        P("batch", "cols", None),
        P("batch", None),
        P("batch", None),
        P("batch", "cols"),
        P("batch", "cols"),
        P("batch", "cols"),
        P("cols", "batch"),
        P("batch"),
        P("batch"),
    )
    out_specs = (
        P(None, "cols"),
        P(None, "cols"),
        P(None, "cols"),
        P("cols", None),
        P(),
        P(),
        P("batch", "cols"),
        P("batch", "cols"),
        P("batch", "cols"),
        P("cols", "batch"),
        P("batch"),
        P("batch"),
    )
    return jax.shard_map(replica_step, mesh=mesh, in_specs=in_specs, out_specs=out_specs, check_vma=False)
```

profile of v0, /device:TPU:0, one launch (start us, length us, event | category | flops | bytes accessed | tf_op | source)
XLA Modules:
  0.0 70.3 jit_solution(17889684134656318605)
XLA Ops:
  1.8 3.0 %collective-permute-start.6 = (f16[256,256]{1,0:T(8,128)(2,1)S(1)}, f16[256,256]{1,0:T(8,128)(2,1)S(1)}, u32[]{:S(2)}, u32[]{:S(2)}) collective-permute-start(f16[256,256]{1,0:T(8,128)(2,1)S(1)} %fusion.43), channel_id=1, source_target_pairs={{0,4},{4,0},{8,12},{12,8},{16,20},{20,16},{24,28},{28,24},{1,5},{5... | collective-permute-start | bytes 393224 | tf_op jit(solution)/shard_map/ppermute | solution.py:278
  4.9 1.6 %collective-permute-start.5 = (f16[272,256]{1,0:T(8,128)(2,1)S(1)}, f16[272,256]{1,0:T(8,128)(2,1)S(1)}, u32[]{:S(2)}, u32[]{:S(2)}) collective-permute-start(f16[272,256]{1,0:T(8,128)(2,1)S(1)} %fusion.38), channel_id=1, source_target_pairs={{0,8},{4,12},{8,0},{12,4},{16,24},{20,28},{24,16},{28,20},{1,9},{5... | collective-permute-start | bytes 417800 | tf_op jit(solution)/shard_map/ppermute | solution.py:278
  6.5 1.6 %shard_map.212 = f32[4,528,256]{2,1,0:T(8,128)S(1)} custom-call(f32[1024,256]{1,0:T(8,128)} %bitcast.86, f32[1024,256]{1,0:T(8,128)} %bitcast.89, f32[1024,256]{1,0:T(8,128)} %bitcast.92, f32[256,1024]{1,0:T(8,128)} %bitcast.95, f32[1,1024]{1,0:T(1,128)} %n.5, f32[1,1024]{1,0:T(1,128)} %b.5), custom_call_target="tpu_custom_call" | custom-call | tf_op jit(solution)/shard_map/pallas_call | solution.py:96
  8.8 1.5 %collective-permute-start.3 = (f16[256,256]{1,0:T(8,128)(2,1)S(1)}, f16[256,256]{1,0:T(8,128)(2,1)S(1)}, u32[]{:S(2)}, u32[]{:S(2)}) collective-permute-start(f16[256,256]{1,0:T(8,128)(2,1)S(1)} %get-tuple-element.59), channel_id=1, source_target_pairs={{0,4},{4,0},{8,12},{12,8},{16,20},{20,16},{24,28},{28,24},{1,5},{5... | collective-permute-start | bytes 393224 | tf_op jit(solution)/shard_map/ppermute | solution.py:278
  10.9 1.4 %shard_map.211 = f32[3,528,256]{2,1,0:T(8,128)S(1)} custom-call(f32[1024,256]{1,0:T(8,128)} %bitcast.87, f32[1024,256]{1,0:T(8,128)} %bitcast.90, f32[1024,256]{1,0:T(8,128)} %bitcast.93, f32[256,1024]{1,0:T(8,128)} %bitcast.96, f32[1,1024]{1,0:T(1,128)} %n.5, f32[1,1024]{1,0:T(1,128)} %b.5), custom_call_target="tpu_custom_call" | custom-call | tf_op jit(solution)/shard_map/pallas_call | solution.py:96
  12.7 2.1 %collective-permute-start.7 = (f16[256,256]{1,0:T(8,128)(2,1)S(1)}, f16[256,256]{1,0:T(8,128)(2,1)S(1)}, u32[]{:S(2)}, u32[]{:S(2)}) collective-permute-start(f16[256,256]{1,0:T(8,128)(2,1)S(1)} %fusion.21), channel_id=1, source_target_pairs={{0,8},{4,12},{8,0},{12,4},{16,24},{20,28},{24,16},{28,20},{1,9},{5... | collective-permute-start | bytes 393224 | tf_op jit(solution)/shard_map/ppermute | solution.py:278
  14.9 1.6 %collective-permute-start = (f16[256,256]{1,0:T(8,128)(2,1)S(1)}, f16[256,256]{1,0:T(8,128)(2,1)S(1)}, u32[]{:S(2)}, u32[]{:S(2)}) collective-permute-start(f16[256,256]{1,0:T(8,128)(2,1)S(1)} %get-tuple-element.57), channel_id=1, source_target_pairs={{0,4},{4,0},{8,12},{12,8},{16,20},{20,16},{24,28},{28,24},{1,5},{5... | collective-permute-start | bytes 393224 | tf_op jit(solution)/shard_map/ppermute | solution.py:278
  16.4 1.7 %collective-permute-done.7 = f16[256,256]{1,0:T(8,128)(2,1)S(1)} collective-permute-done((f16[256,256]{1,0:T(8,128)(2,1)S(1)}, f16[256,256]{1,0:T(8,128)(2,1)S(1)}, u32[]{:S(2)}, u32[]{:S(2)}) %collective-permute-start.7) | collective-permute-done | bytes 131104 | tf_op jit(solution)/shard_map/ppermute | solution.py:278
  18.1 1.5 %collective-permute-start.20 = (f16[272,256]{1,0:T(8,128)(2,1)S(1)}, f16[272,256]{1,0:T(8,128)(2,1)S(1)}, u32[]{:S(2)}, u32[]{:S(2)}) collective-permute-start(f16[272,256]{1,0:T(8,128)(2,1)S(1)} %get-tuple-element.54), channel_id=1, source_target_pairs={{0,4},{4,0},{8,12},{12,8},{16,20},{20,16},{24,28},{28,24},{1,5},{5... | collective-permute-start | bytes 417800 | tf_op jit(solution)/shard_map/ppermute | solution.py:278
  20.4 1.7 %collective-permute-start.10 = (f16[256,256]{1,0:T(8,128)(2,1)S(1)}, f16[256,256]{1,0:T(8,128)(2,1)S(1)}, u32[]{:S(2)}, u32[]{:S(2)}) collective-permute-start(f16[256,256]{1,0:T(8,128)(2,1)S(1)} %fusion.30), channel_id=1, source_target_pairs={{0,8},{4,12},{8,0},{12,4},{16,24},{20,28},{24,16},{28,20},{1,9},{5... | collective-permute-start | bytes 393224 | tf_op jit(solution)/shard_map/ppermute | solution.py:278
  22.1 5.4 %collective-permute-done.8 = f16[272,256]{1,0:T(8,128)(2,1)S(1)} collective-permute-done((f16[272,256]{1,0:T(8,128)(2,1)S(1)}, f16[272,256]{1,0:T(8,128)(2,1)S(1)}, u32[]{:S(2)}, u32[]{:S(2)}) %collective-permute-start.8) | collective-permute-done | bytes 139296 | tf_op jit(solution)/shard_map/ppermute | solution.py:278
  27.5 2.6 %collective-permute-start.9 = (f16[256,256]{1,0:T(8,128)(2,1)S(1)}, f16[256,256]{1,0:T(8,128)(2,1)S(1)}, u32[]{:S(2)}, u32[]{:S(2)}) collective-permute-start(f16[256,256]{1,0:T(8,128)(2,1)S(1)} %fusion.26), channel_id=1, source_target_pairs={{0,16},{4,20},{8,24},{12,28},{16,0},{20,4},{24,8},{28,12},{1,17},{... | collective-permute-start | bytes 393224 | tf_op jit(solution)/shard_map/ppermute | solution.py:278
  31.2 7.9 %collective-permute-done.9 = f16[256,256]{1,0:T(8,128)(2,1)S(1)} collective-permute-done((f16[256,256]{1,0:T(8,128)(2,1)S(1)}, f16[256,256]{1,0:T(8,128)(2,1)S(1)}, u32[]{:S(2)}, u32[]{:S(2)}) %collective-permute-start.9) | collective-permute-done | bytes 131104 | tf_op jit(solution)/shard_map/ppermute | solution.py:278
  40.0 3.0 %collective-permute-start.12 = (bf16[256,256]{1,0:T(8,128)(2,1)S(1)}, bf16[256,256]{1,0:T(8,128)(2,1)S(1)}, u32[]{:S(2)}, u32[]{:S(2)}) collective-permute-start(bf16[256,256]{1,0:T(8,128)(2,1)S(1)} %get-tuple-element.39.refs_0_), channel_id=1, source_target_pairs={{0,8},{4,12},{8,0},{12,4},{16,24},{20,28},{24,16},{28,20},{1,9},{5... | collective-permute-start | bytes 393224 | tf_op jit(solution)/shard_map/ppermute | solution.py:278
  44.8 5.7 %collective-permute-start.22 = (bf16[272,256]{1,0:T(8,128)(2,1)S(1)}, bf16[272,256]{1,0:T(8,128)(2,1)S(1)}, u32[]{:S(2)}, u32[]{:S(2)}) collective-permute-start(bf16[272,256]{1,0:T(8,128)(2,1)S(1)} %get-tuple-element.43.refs_0_), channel_id=1, source_target_pairs={{0,8},{4,12},{8,0},{12,4},{16,24},{20,28},{24,16},{28,20},{1,9},{5... | collective-permute-start | bytes 417800 | tf_op jit(solution)/shard_map/ppermute | solution.py:278
  50.5 2.0 %collective-permute-start.15 = (bf16[256,256]{1,0:T(8,128)(2,1)S(1)}, bf16[256,256]{1,0:T(8,128)(2,1)S(1)}, u32[]{:S(2)}, u32[]{:S(2)}) collective-permute-start(bf16[256,256]{1,0:T(8,128)(2,1)S(1)} %collective-permute-done.14.refs_4_), channel_id=1, source_target_pairs={{0,4},{4,0},{8,12},{12,8},{16,20},{20,16},{24,28},{28,24},{1,5},{5... | collective-permute-start | bytes 393224 | tf_op jit(solution)/shard_map/ppermute | solution.py:278
  52.7 2.0 %collective-permute-start.26 = (bf16[272,256]{1,0:T(8,128)(2,1)S(1)}, bf16[272,256]{1,0:T(8,128)(2,1)S(1)}, u32[]{:S(2)}, u32[]{:S(2)}) collective-permute-start(bf16[272,256]{1,0:T(8,128)(2,1)S(1)} %collective-permute-done.24.refs_4_), channel_id=1, source_target_pairs={{0,8},{4,12},{8,0},{12,4},{16,24},{20,28},{24,16},{28,20},{1,9},{5... | collective-permute-start | bytes 417800 | tf_op jit(solution)/shard_map/ppermute | solution.py:278
  55.0 1.9 %collective-permute-start.21 = (bf16[272,256]{1,0:T(8,128)(2,1)S(1)}, bf16[272,256]{1,0:T(8,128)(2,1)S(1)}, u32[]{:S(2)}, u32[]{:S(2)}) collective-permute-start(bf16[272,256]{1,0:T(8,128)(2,1)S(1)} %get-tuple-element.43.refs_0_), channel_id=1, source_target_pairs={{0,4},{4,0},{8,12},{12,8},{16,20},{20,16},{24,28},{28,24},{1,5},{5... | collective-permute-start | bytes 417800 | tf_op jit(solution)/shard_map/ppermute | solution.py:278
  56.9 1.9 %collective-permute-start.25 = (bf16[272,256]{1,0:T(8,128)(2,1)S(1)}, bf16[272,256]{1,0:T(8,128)(2,1)S(1)}, u32[]{:S(2)}, u32[]{:S(2)}) collective-permute-start(bf16[272,256]{1,0:T(8,128)(2,1)S(1)} %collective-permute-done.24.refs_4_), channel_id=1, source_target_pairs={{0,4},{4,0},{8,12},{12,8},{16,20},{20,16},{24,28},{28,24},{1,5},{5... | collective-permute-start | bytes 417800 | tf_op jit(solution)/shard_map/ppermute | solution.py:278
  59.5 2.2 %collective-permute-start.23 = (bf16[272,256]{1,0:T(8,128)(2,1)S(1)}, bf16[272,256]{1,0:T(8,128)(2,1)S(1)}, u32[]{:S(2)}, u32[]{:S(2)}) collective-permute-start(bf16[272,256]{1,0:T(8,128)(2,1)S(1)} %collective-permute-done.22.refs_2_), channel_id=1, source_target_pairs={{0,4},{4,0},{8,12},{12,8},{16,20},{20,16},{24,28},{28,24},{1,5},{5... | collective-permute-start | bytes 417800 | tf_op jit(solution)/shard_map/ppermute | solution.py:278
  61.8 1.2 %collective-permute-start.27 = (bf16[272,256]{1,0:T(8,128)(2,1)S(1)}, bf16[272,256]{1,0:T(8,128)(2,1)S(1)}, u32[]{:S(2)}, u32[]{:S(2)}) collective-permute-start(bf16[272,256]{1,0:T(8,128)(2,1)S(1)} %collective-permute-done.26.refs_6_), channel_id=1, source_target_pairs={{0,4},{4,0},{8,12},{12,8},{16,20},{20,16},{24,28},{28,24},{1,5},{5... | collective-permute-start | bytes 417800 | tf_op jit(solution)/shard_map/ppermute | solution.py:278
  62.9 3.7 %collective-permute-done.17.refs_7_ = bf16[256,256]{1,0:T(8,128)(2,1)S(1)} collective-permute-done((bf16[256,256]{1,0:T(8,128)(2,1)S(1)}, bf16[256,256]{1,0:T(8,128)(2,1)S(1)}, u32[]{:S(2)}, u32[]{:S(2)}) %collective-permute-start.17) | collective-permute-done | bytes 131104 | tf_op jit(solution)/shard_map/ppermute | solution.py:278
  67.6 1.1 %collective-permute-done.27.refs_7_ = bf16[272,256]{1,0:T(8,128)(2,1)S(1)} collective-permute-done((bf16[272,256]{1,0:T(8,128)(2,1)S(1)}, bf16[272,256]{1,0:T(8,128)(2,1)S(1)}, u32[]{:S(2)}, u32[]{:S(2)}) %collective-permute-start.27) | collective-permute-done | bytes 139296 | tf_op jit(solution)/shard_map/ppermute | solution.py:278
  68.8 1.5 %unpack.3 = (bf16[1024,256]{1,0:T(8,128)(2,1)}, bf16[256,1024]{1,0:T(8,128)(2,1)}, bf16[8,128]{1,0:T(8,128)(2,1)}, bf16[8,128]{1,0:T(8,128)(2,1)}) custom-call(bf16[272,256]{1,0:T(8,128)(2,1)S(1)} %get-tuple-element.43.refs_0_, bf16[272,256]{1,0:T(8,128)(2,1)S(1)} %collective-permute-done.21.refs_1_, bf16[272,256]{1,0:T(8,128)(2,1)S(1)} %collective-permute-done.22.refs_2_, ...), custom_call_target="tpu_custom_call" | custom-call | tf_op jit(solution)/shard_map/unpack/pallas_call | solution.py:195
  (77 shorter events, 9.2 us)
Async XLA Ops:
  1.8 10.7 %collective-permute-start.6 = (f16[256,256]{1,0:T(8,128)(2,1)S(1)}, f16[256,256]{1,0:T(8,128)(2,1)S(1)}, u32[]{:S(2)}, u32[]{:S(2)}) collective-permute-start(f16[256,256]{1,0:T(8,128)(2,1)S(1)} %fusion.43), channel_id=1, source_target_pairs={{0,4},{4,0},{8,12},{12,8},{16,20},{20,16},{24,28},{28,24},{1,5},{5... | collective-permute-start | bytes 393224 | tf_op jit(solution)/shard_map/ppermute | solution.py:278
  4.9 7.9 %collective-permute-start.5 = (f16[272,256]{1,0:T(8,128)(2,1)S(1)}, f16[272,256]{1,0:T(8,128)(2,1)S(1)}, u32[]{:S(2)}, u32[]{:S(2)}) collective-permute-start(f16[272,256]{1,0:T(8,128)(2,1)S(1)} %fusion.38), channel_id=1, source_target_pairs={{0,8},{4,12},{8,0},{12,4},{16,24},{20,28},{24,16},{28,20},{1,9},{5... | collective-permute-start | bytes 417800 | tf_op jit(solution)/shard_map/ppermute | solution.py:278
  8.8 11.0 %collective-permute-start.3 = (f16[256,256]{1,0:T(8,128)(2,1)S(1)}, f16[256,256]{1,0:T(8,128)(2,1)S(1)}, u32[]{:S(2)}, u32[]{:S(2)}) collective-permute-start(f16[256,256]{1,0:T(8,128)(2,1)S(1)} %get-tuple-element.59), channel_id=1, source_target_pairs={{0,4},{4,0},{8,12},{12,8},{16,20},{20,16},{24,28},{28,24},{1,5},{5... | collective-permute-start | bytes 393224 | tf_op jit(solution)/shard_map/ppermute | solution.py:278
  10.4 10.0 %collective-permute-start.2 = (f16[272,256]{1,0:T(8,128)(2,1)S(1)}, f16[272,256]{1,0:T(8,128)(2,1)S(1)}, u32[]{:S(2)}, u32[]{:S(2)}) collective-permute-start(f16[272,256]{1,0:T(8,128)(2,1)S(1)} %get-tuple-element.55), channel_id=1, source_target_pairs={{0,8},{4,12},{8,0},{12,4},{16,24},{20,28},{24,16},{28,20},{1,9},{5... | collective-permute-start | bytes 417800 | tf_op jit(solution)/shard_map/ppermute | solution.py:278
  12.5 17.7 %collective-permute-start.1 = (f16[272,256]{1,0:T(8,128)(2,1)S(1)}, f16[272,256]{1,0:T(8,128)(2,1)S(1)}, u32[]{:S(2)}, u32[]{:S(2)}) collective-permute-start(f16[272,256]{1,0:T(8,128)(2,1)S(1)} %get-tuple-element.56), channel_id=1, source_target_pairs={{0,4},{4,0},{8,12},{12,8},{16,20},{20,16},{24,28},{28,24},{1,5},{5... | collective-permute-start | bytes 417800 | tf_op jit(solution)/shard_map/ppermute | solution.py:278
  14.9 15.8 %collective-permute-start = (f16[256,256]{1,0:T(8,128)(2,1)S(1)}, f16[256,256]{1,0:T(8,128)(2,1)S(1)}, u32[]{:S(2)}, u32[]{:S(2)}) collective-permute-start(f16[256,256]{1,0:T(8,128)(2,1)S(1)} %get-tuple-element.57), channel_id=1, source_target_pairs={{0,4},{4,0},{8,12},{12,8},{16,20},{20,16},{24,28},{28,24},{1,5},{5... | collective-permute-start | bytes 393224 | tf_op jit(solution)/shard_map/ppermute | solution.py:278
  18.1 25.8 %collective-permute-start.20 = (f16[272,256]{1,0:T(8,128)(2,1)S(1)}, f16[272,256]{1,0:T(8,128)(2,1)S(1)}, u32[]{:S(2)}, u32[]{:S(2)}) collective-permute-start(f16[272,256]{1,0:T(8,128)(2,1)S(1)} %get-tuple-element.54), channel_id=1, source_target_pairs={{0,4},{4,0},{8,12},{12,8},{16,20},{20,16},{24,28},{28,24},{1,5},{5... | collective-permute-start | bytes 417800 | tf_op jit(solution)/shard_map/ppermute | solution.py:278
  19.8 7.7 %collective-permute-start.8 = (f16[272,256]{1,0:T(8,128)(2,1)S(1)}, f16[272,256]{1,0:T(8,128)(2,1)S(1)}, u32[]{:S(2)}, u32[]{:S(2)}) collective-permute-start(f16[272,256]{1,0:T(8,128)(2,1)S(1)} %fusion.8), channel_id=1, source_target_pairs={{0,4},{4,0},{8,12},{12,8},{16,20},{20,16},{24,28},{28,24},{1,5},{5... | collective-permute-start | bytes 417800 | tf_op jit(solution)/shard_map/ppermute | solution.py:278
  20.4 10.8 %collective-permute-start.10 = (f16[256,256]{1,0:T(8,128)(2,1)S(1)}, f16[256,256]{1,0:T(8,128)(2,1)S(1)}, u32[]{:S(2)}, u32[]{:S(2)}) collective-permute-start(f16[256,256]{1,0:T(8,128)(2,1)S(1)} %fusion.30), channel_id=1, source_target_pairs={{0,8},{4,12},{8,0},{12,4},{16,24},{20,28},{24,16},{28,20},{1,9},{5... | collective-permute-start | bytes 393224 | tf_op jit(solution)/shard_map/ppermute | solution.py:278
  27.5 11.6 %collective-permute-start.9 = (f16[256,256]{1,0:T(8,128)(2,1)S(1)}, f16[256,256]{1,0:T(8,128)(2,1)S(1)}, u32[]{:S(2)}, u32[]{:S(2)}) collective-permute-start(f16[256,256]{1,0:T(8,128)(2,1)S(1)} %fusion.26), channel_id=1, source_target_pairs={{0,16},{4,20},{8,24},{12,28},{16,0},{20,4},{24,8},{28,12},{1,17},{... | collective-permute-start | bytes 393224 | tf_op jit(solution)/shard_map/ppermute | solution.py:278
  30.2 13.1 %collective-permute-start.18 = (f16[272,256]{1,0:T(8,128)(2,1)S(1)}, f16[272,256]{1,0:T(8,128)(2,1)S(1)}, u32[]{:S(2)}, u32[]{:S(2)}) collective-permute-start(f16[272,256]{1,0:T(8,128)(2,1)S(1)} %fusion.13), channel_id=1, source_target_pairs={{0,16},{4,20},{8,24},{12,28},{16,0},{20,4},{24,8},{28,12},{1,17},{... | collective-permute-start | bytes 417800 | tf_op jit(solution)/shard_map/ppermute | solution.py:278
  30.7 13.3 %collective-permute-start.19 = (f16[272,256]{1,0:T(8,128)(2,1)S(1)}, f16[272,256]{1,0:T(8,128)(2,1)S(1)}, u32[]{:S(2)}, u32[]{:S(2)}) collective-permute-start(f16[272,256]{1,0:T(8,128)(2,1)S(1)} %fusion.17), channel_id=1, source_target_pairs={{0,8},{4,12},{8,0},{12,4},{16,24},{20,28},{24,16},{28,20},{1,9},{5... | collective-permute-start | bytes 417800 | tf_op jit(solution)/shard_map/ppermute | solution.py:278
  40.0 10.5 %collective-permute-start.14 = (bf16[256,256]{1,0:T(8,128)(2,1)S(1)}, bf16[256,256]{1,0:T(8,128)(2,1)S(1)}, u32[]{:S(2)}, u32[]{:S(2)}) collective-permute-start(bf16[256,256]{1,0:T(8,128)(2,1)S(1)} %get-tuple-element.39.refs_0_), channel_id=1, source_target_pairs={{0,16},{4,20},{8,24},{12,28},{16,0},{20,4},{24,8},{28,12},{1,17},{... | collective-permute-start | bytes 393224 | tf_op jit(solution)/shard_map/ppermute | solution.py:278
  40.0 12.5 %collective-permute-start.12 = (bf16[256,256]{1,0:T(8,128)(2,1)S(1)}, bf16[256,256]{1,0:T(8,128)(2,1)S(1)}, u32[]{:S(2)}, u32[]{:S(2)}) collective-permute-start(bf16[256,256]{1,0:T(8,128)(2,1)S(1)} %get-tuple-element.39.refs_0_), channel_id=1, source_target_pairs={{0,8},{4,12},{8,0},{12,4},{16,24},{20,28},{24,16},{28,20},{1,9},{5... | collective-permute-start | bytes 393224 | tf_op jit(solution)/shard_map/ppermute | solution.py:278
  43.3 9.3 %collective-permute-start.11 = (bf16[256,256]{1,0:T(8,128)(2,1)S(1)}, bf16[256,256]{1,0:T(8,128)(2,1)S(1)}, u32[]{:S(2)}, u32[]{:S(2)}) collective-permute-start(bf16[256,256]{1,0:T(8,128)(2,1)S(1)} %get-tuple-element.39.refs_0_), channel_id=1, source_target_pairs={{0,4},{4,0},{8,12},{12,8},{16,20},{20,16},{24,28},{28,24},{1,5},{5... | collective-permute-start | bytes 393224 | tf_op jit(solution)/shard_map/ppermute | solution.py:278
  44.8 7.9 %collective-permute-start.24 = (bf16[272,256]{1,0:T(8,128)(2,1)S(1)}, bf16[272,256]{1,0:T(8,128)(2,1)S(1)}, u32[]{:S(2)}, u32[]{:S(2)}) collective-permute-start(bf16[272,256]{1,0:T(8,128)(2,1)S(1)} %get-tuple-element.43.refs_0_), channel_id=1, source_target_pairs={{0,16},{4,20},{8,24},{12,28},{16,0},{20,4},{24,8},{28,12},{1,17},{... | collective-permute-start | bytes 417800 | tf_op jit(solution)/shard_map/ppermute | solution.py:278
  44.8 10.2 %collective-permute-start.22 = (bf16[272,256]{1,0:T(8,128)(2,1)S(1)}, bf16[272,256]{1,0:T(8,128)(2,1)S(1)}, u32[]{:S(2)}, u32[]{:S(2)}) collective-permute-start(bf16[272,256]{1,0:T(8,128)(2,1)S(1)} %get-tuple-element.43.refs_0_), channel_id=1, source_target_pairs={{0,8},{4,12},{8,0},{12,4},{16,24},{20,28},{24,16},{28,20},{1,9},{5... | collective-permute-start | bytes 417800 | tf_op jit(solution)/shard_map/ppermute | solution.py:278
  52.5 9.2 %collective-permute-start.16 = (bf16[256,256]{1,0:T(8,128)(2,1)S(1)}, bf16[256,256]{1,0:T(8,128)(2,1)S(1)}, u32[]{:S(2)}, u32[]{:S(2)}) collective-permute-start(bf16[256,256]{1,0:T(8,128)(2,1)S(1)} %collective-permute-done.14.refs_4_), channel_id=1, source_target_pairs={{0,8},{4,12},{8,0},{12,4},{16,24},{20,28},{24,16},{28,20},{1,9},{5... | collective-permute-start | bytes 393224 | tf_op jit(solution)/shard_map/ppermute | solution.py:278
  52.6 6.9 %collective-permute-start.13 = (bf16[256,256]{1,0:T(8,128)(2,1)S(1)}, bf16[256,256]{1,0:T(8,128)(2,1)S(1)}, u32[]{:S(2)}, u32[]{:S(2)}) collective-permute-start(bf16[256,256]{1,0:T(8,128)(2,1)S(1)} %collective-permute-done.12.refs_2_), channel_id=1, source_target_pairs={{0,4},{4,0},{8,12},{12,8},{16,20},{20,16},{24,28},{28,24},{1,5},{5... | collective-permute-start | bytes 393224 | tf_op jit(solution)/shard_map/ppermute | solution.py:278
  52.7 9.1 %collective-permute-start.26 = (bf16[272,256]{1,0:T(8,128)(2,1)S(1)}, bf16[272,256]{1,0:T(8,128)(2,1)S(1)}, u32[]{:S(2)}, u32[]{:S(2)}) collective-permute-start(bf16[272,256]{1,0:T(8,128)(2,1)S(1)} %collective-permute-done.24.refs_4_), channel_id=1, source_target_pairs={{0,8},{4,12},{8,0},{12,4},{16,24},{20,28},{24,16},{28,20},{1,9},{5... | collective-permute-start | bytes 417800 | tf_op jit(solution)/shard_map/ppermute | solution.py:278
  55.0 12.6 %collective-permute-start.21 = (bf16[272,256]{1,0:T(8,128)(2,1)S(1)}, bf16[272,256]{1,0:T(8,128)(2,1)S(1)}, u32[]{:S(2)}, u32[]{:S(2)}) collective-permute-start(bf16[272,256]{1,0:T(8,128)(2,1)S(1)} %get-tuple-element.43.refs_0_), channel_id=1, source_target_pairs={{0,4},{4,0},{8,12},{12,8},{16,20},{20,16},{24,28},{28,24},{1,5},{5... | collective-permute-start | bytes 417800 | tf_op jit(solution)/shard_map/ppermute | solution.py:278
  56.9 10.7 %collective-permute-start.25 = (bf16[272,256]{1,0:T(8,128)(2,1)S(1)}, bf16[272,256]{1,0:T(8,128)(2,1)S(1)}, u32[]{:S(2)}, u32[]{:S(2)}) collective-permute-start(bf16[272,256]{1,0:T(8,128)(2,1)S(1)} %collective-permute-done.24.refs_4_), channel_id=1, source_target_pairs={{0,4},{4,0},{8,12},{12,8},{16,20},{20,16},{24,28},{28,24},{1,5},{5... | collective-permute-start | bytes 417800 | tf_op jit(solution)/shard_map/ppermute | solution.py:278
  59.5 8.2 %collective-permute-start.23 = (bf16[272,256]{1,0:T(8,128)(2,1)S(1)}, bf16[272,256]{1,0:T(8,128)(2,1)S(1)}, u32[]{:S(2)}, u32[]{:S(2)}) collective-permute-start(bf16[272,256]{1,0:T(8,128)(2,1)S(1)} %collective-permute-done.22.refs_2_), channel_id=1, source_target_pairs={{0,4},{4,0},{8,12},{12,8},{16,20},{20,16},{24,28},{28,24},{1,5},{5... | collective-permute-start | bytes 417800 | tf_op jit(solution)/shard_map/ppermute | solution.py:278
  61.8 7.0 %collective-permute-start.27 = (bf16[272,256]{1,0:T(8,128)(2,1)S(1)}, bf16[272,256]{1,0:T(8,128)(2,1)S(1)}, u32[]{:S(2)}, u32[]{:S(2)}) collective-permute-start(bf16[272,256]{1,0:T(8,128)(2,1)S(1)} %collective-permute-done.26.refs_6_), channel_id=1, source_target_pairs={{0,4},{4,0},{8,12},{12,8},{16,20},{20,16},{24,28},{28,24},{1,5},{5... | collective-permute-start | bytes 417800 | tf_op jit(solution)/shard_map/ppermute | solution.py:278
  (10 other events, 109.3 us)
where the time goes:
time: 70.5 us; the launch traced here: 70.3 us
  starting transfers between devices  39.2 us (56%)
  waiting for transfers between devices  21.2 us (30%)
  Pallas kernels  8.09 us (11%)
  between operations  0.99 us (1%)
  other arithmetic  0.79 us (1%)
    ppermute x28, starting transfers between devices, swap(): return lax.ppermute(x, 'batch', [(i, i ^ bit) for i in range(replicas)])  39.2 us
    ppermute x28, waiting for transfers between devices, swap(): return lax.ppermute(x, 'batch', [(i, i ^ bit) for i in range(replicas)])  21.2 us
    pallas_call x3, Pallas kernels, pack_tiles(): pl.pallas_call(kernel, out_shape=jax.ShapeDtypeStruct((len(offsets), heig...  4.15 us
    pallas_call x2, Pallas kernels, unpack_tiles(): pl.pallas_call(kernel, out_shape=[jax.ShapeDtypeStruct(shapes[p], jnp.bfl...  2.49 us
    pallas_call x2, Pallas kernels, step_tiles(): pl.pallas_call(kernel, out_shape=[jax.ShapeDtypeStruct((height + tail, co...  1.45 us
  transfers between devices with their start and end apart: 28, of which 8 were waited for; matrix products, arithmetic and copies ran while one was open for 1% of the time, Pallas kernels for 8%

commit v1 on v0

--- a/solution.py
+++ b/solution.py
@@ -10,7 +10,7 @@
 
 learn_rate = 0.4
 lanes = 128
-tail_rows = 16
+tail_rows = 8
 vmem_grant = 16 << 20
 largest_partial = 12.0
 
@@ -156,18 +156,23 @@
     return slab, [x if p < 4 else x.reshape(-1) for p, x in zip(parts, own)]
 
 
-def unpack_tiles(pieces, tick, parts, rows, cols):
-    replicas = len(pieces)
+def unpack_tiles(pieces, begun, tick, parts, rows, cols, replicas):
     height = rows * sum(p < 4 for p in parts)
     vectors = [p for p in parts if p > 3]
+    slabs = sorted(pieces)
+    ends = not begun and len(slabs) == replicas or bool(begun)
+    lines_out = [(replicas, rows)] * len(vectors)
 
     def kernel(*refs):
-        got, outs = refs[:replicas], refs[replicas + 1 : replicas + 1 + len(parts)]
-        *lines, sem = refs[replicas + 1 + len(parts) :]
-        here = lax.axis_index("batch")
+        refs = list(refs)
+        got = [refs.pop(0) for _ in slabs]
+        refs.pop(0)
+        earlier = [refs.pop(0) for _ in begun]
+        outs = [refs.pop(0) for _ in parts]
+        *lines, sem = refs
         started = []
-        for j, piece in enumerate(got):
-            start = pl.multiple_of((here ^ j) * rows, lanes)
+        for j, piece in zip(slabs, got):
+            start = pl.multiple_of((lax.axis_index("batch") ^ j) * rows, lanes)
             for i, (p, out) in enumerate(zip(parts, outs)):
                 at = pl.ds(i * rows, rows)
                 if p < 3:
@@ -180,28 +185,33 @@
                 started += [pltpu.make_async_copy(*pair, sem.at[0]) for pair in pairs]
         for c in started:
             c.start()
-        for j, piece in enumerate(got):
+        for line, old in zip(lines, earlier[len(parts) - len(vectors) :]):
+            line[...] = old[...]
+        for j, piece in zip(slabs, got):
             for p, line in zip(vectors, lines):
                 tail = piece[pl.ds(height, tail_rows), pl.ds((p - 4) * rows, rows)]
-                line[pl.ds(here ^ j, 1), :] = tail.astype(jnp.float32)[0:1]
+                line[pl.ds(lax.axis_index("batch") ^ j, 1), :] = tail.astype(jnp.float32)[0:1]
         for line, out in zip(lines, outs[len(parts) - len(vectors) :]):
-            out[...] = line[...].astype(jnp.bfloat16)
+            out[...] = line[...].astype(out.dtype)
         for c in started:
             c.wait()
 
     shapes = [(replicas * rows, cols)] * 3 + [(cols, replicas * rows)] + [(replicas, rows)] * 2
+    kinds = [jnp.bfloat16 if p < 4 or ends else jnp.float32 for p in parts]
     hbm = pl.BlockSpec(memory_space=pltpu.HBM)
     vmem = pl.BlockSpec(memory_space=pltpu.VMEM)
+    spaces = [hbm if p < 4 else vmem for p in parts]
     outs = pl.pallas_call(
         kernel,
-        out_shape=[jax.ShapeDtypeStruct(shapes[p], jnp.bfloat16) for p in parts],
-        in_specs=[vmem] * (replicas + 1),
-        out_specs=[hbm if p < 4 else vmem for p in parts],
-        scratch_shapes=[pltpu.VMEM((replicas, rows), jnp.float32) for _ in vectors] + [pltpu.SemaphoreType.DMA((1,))],
+        out_shape=[jax.ShapeDtypeStruct(shapes[p], kind) for p, kind in zip(parts, kinds)],
+        in_specs=[vmem] * (len(slabs) + 1) + (spaces if begun else []),
+        out_specs=spaces,
+        scratch_shapes=[pltpu.VMEM(x, jnp.float32) for x in lines_out] + [pltpu.SemaphoreType.DMA((1,))],
+        input_output_aliases={len(slabs) + 1 + i: i for i, p in enumerate(parts) if p < 4} if begun else {},
         name="unpack",
         compiler_params=pltpu.CompilerParams(vmem_limit_bytes=vmem_grant),
-    )(*pieces, tick)
-    return [x if p < 4 else x.reshape(-1) for p, x in zip(parts, outs)]
+    )(*[pieces[j] for j in slabs], tick, *begun)
+    return [x if p < 4 or not ends else x.reshape(-1) for p, x in zip(parts, outs)]
 
 
 def unpack_plain(pieces, rows, cols, replicas):
@@ -216,13 +226,13 @@
 
 
 order_of_8 = (
-    (0, 7, 0), (0, 7, 1), (0, 5, 0), (0, 6, 1), (0, 3, 0), (0, 6, 0), (0, 5, 1), (0, 1, 0), (0, 3, 1),
-    (0, 4, 0), (0, 2, 0), (0, 4, 1), (0, 2, 1), (0, 1, 1), (1, 4, 0), (1, 1, 0), (1, 2, 0), (1, 4, 1),
-    (1, 1, 1), (1, 2, 1), (1, 3, 0), (1, 5, 0), (1, 5, 1), (1, 6, 0), (1, 3, 1), (1, 6, 1), (1, 7, 0),
-    (1, 7, 1),
+    ((0, 7, 0),), ((0, 5, 0),), ((0, 7, 1),), ((0, 3, 0),), ((0, 6, 0),), ((0, 6, 1),), ((0, 5, 1),),
+    ((0, 3, 1),), ((0, 1, 0),), ((0, 4, 0),), ((0, 2, 0),), ((0, 4, 1),), ((0, 2, 1),), ((0, 1, 1),),
+    ((1, 4, 0),), ((1, 1, 0),), ((1, 2, 0),), ((1, 1, 1),), ((1, 4, 1),), ((1, 2, 1),), ((1, 3, 0),),
+    ((1, 5, 0),), ((1, 5, 1),), ((1, 6, 1),), ((1, 6, 0),), ((1, 3, 1),), ((1, 7, 0),), ((1, 7, 1),),
 )
 bits_of_8 = {(0, 7, 1): 2, (1, 7, 0): 2}
-packs_of_8 = ((7,), (6, 5, 3, 1,), (4, 2, 0,))
+packs_of_8 = ((7, 5, 3), (6, 1, 4, 2, 0))
 
 
 def plan_of(replicas, fits):
@@ -234,7 +244,8 @@
         return groups, bits, list(order_of_8)
     chunks = [*range(replicas - 1, 0, -2), *range(replicas - 2, 0, -2)]
     back = sorted(range(1, replicas), key=lambda j: (j & 1, j.bit_count(), j))
-    return groups, bits, [(w, j, g) for w, order in ((0, chunks), (1, back)) for j in order for g in range(len(groups))]
+    order = [((w, j, g),) for w, js in ((0, chunks), (1, back)) for j in js for g in range(len(groups))]
+    return groups, bits, order
 
 
 def inputs_of(at, bits):
@@ -248,11 +259,15 @@
 
 def ticks_of(bits, order):
     late, seen = {}, set()
-    for before, at in zip(order, order[1:]):
-        new = [k for k in inputs_of(at, bits) if k not in seen]
+    home = {at: exchange for exchange in order for at in exchange}
+    for before, exchange in zip(order, order[1:]):
+        new = []
+        for at in exchange:
+            new += [home[k] for k in inputs_of(at, bits) if home[k] not in seen and home[k] not in new]
         seen.update(new)
-        if new and new != [before]:
-            late[before] = [k for k in new if k != before]
+        new = [k for k in new if k != before]
+        if new:
+            late[before] = new
     return late
 
 
@@ -274,8 +289,12 @@
     else:
         slabs = dict(zip(every, pack_plain(partials, [here ^ j for j in every], replicas, here)))
 
-    def swap(x, bit):
-        return lax.ppermute(x, "batch", [(i, i ^ bit) for i in range(replicas)])
+    def swap(xs, exchange):
+        (bit,) = {bits[at] for at in exchange}
+        x = xs[0] if len(xs) == 1 else jnp.concatenate(xs)
+        x = lax.ppermute(x, "batch", [(i, i ^ bit) for i in every])
+        ends = [sum(y.shape[0] for y in xs[: i + 1]) for i in range(len(xs))]
+        return [x] if len(xs) == 1 else [x[end - y.shape[0] : end] for end, y in zip(ends, xs)]
 
     tall = slabs[0].shape[0]
     bounds = []
@@ -299,27 +318,38 @@
     ticks = ticks_of(bits, order) if fits else {}
     tick = masters[4][None]
     own, full, pieces = [None] * 6, [None] * 6, {}
-    for at in order:
-        w, j, g = at
-        bit = bits[at]
-        if w == 0:
-            send = total(j, g).astype(jnp.float16)
-            if got[j, g]:
-                ahead = send
-            got[j ^ bit, g].append(swap(send, bit))
-        else:
+    for exchange in order:
+        sends = []
+        for w, j, g in exchange:
+            if w == 0:
+                sends.append(total(j, g).astype(jnp.float16))
+                if got[j, g]:
+                    ahead = sends[-1]
+                continue
             if (0, g) not in pieces:
                 ahead = total(0, g)
                 step = step_tiles if fits else step_plain
                 pieces[0, g], new = step(ahead, masters, groups[g], rate, rows, cols)
                 for p, x in zip(groups[g], new):
                     own[p] = x
-            pieces[j, g] = swap(pieces[j ^ bit, g], bit)
-        if at in ticks:
+            sends.append(pieces[j ^ bits[w, j, g], g])
+        for (w, j, g), x in zip(exchange, swap(sends, exchange)):
+            if w == 0:
+                got[j ^ bits[w, j, g], g].append(x)
+            else:
+                pieces[j, g] = x
+        if exchange in ticks:
             tick = lax.optimization_barrier(tick) + 1.0
     for g, parts in enumerate(groups):
-        mine = [pieces[j, g] for j in range(replicas)]
-        done = unpack_tiles(mine, tick, parts, rows, cols) if fits else unpack_plain(mine, rows, cols, replicas)
+        mine = {j: pieces[j, g] for j in range(replicas)}
+        if not fits:
+            done = unpack_plain([mine[j] for j in range(replicas)], rows, cols, replicas)
+        elif g == order[-1][-1][2]:
+            last = {at[1]: mine.pop(at[1]) for at in order[-1]}
+            done = unpack_tiles(mine, [], tick, parts, rows, cols, replicas)
+            done = unpack_tiles(last, done, tick, parts, rows, cols, replicas)
+        else:
+            done = unpack_tiles(mine, [], tick, parts, rows, cols, replicas)
         for p, x in zip(parts, done):
             full[p] = x
     return (*full, *own)

time: 70.5 us -> 73.8 us (1.047)
  waiting for transfers between devices: 21.2 us -> 27.8 us
  starting transfers between devices: 39.2 us -> 36.3 us
    ppermute x28, waiting for transfers between devices: 21.2 us -> 27.8 us  [swap(): x = lax.ppermute(x, 'batch', [(i, i ^ bit) for i in every])]
    ppermute x28, starting transfers between devices: 39.2 us -> 36.3 us  [swap(): x = lax.ppermute(x, 'batch', [(i, i ^ bit) for i in every])]
    pallas_call x3 -> x2, Pallas kernels: 4.15 us -> 3.22 us  [pack_tiles(): pl.pallas_call(kernel, out_shape=jax.ShapeDtypeStruct((len(offsets), heig...]
    pallas_call x2 -> x3, Pallas kernels: 2.49 us -> 3.1 us  [unpack_tiles(): pl.pallas_call(kernel, out_shape=[jax.ShapeDtypeStruct(shapes[p], kind) f...]
  transfers between devices with their start and end apart: 28 -> 28, of which waited for: 8 -> 9; matrix products, arithmetic and copies ran while one was open for 1% -> 1% of each run, Pallas kernels for 8% -> 7%
where the time goes in v1:
time: 73.8 us; the launch traced here: 73.6 us
  starting transfers between devices  36.3 us (49%)
  waiting for transfers between devices  27.8 us (38%)
  Pallas kernels  7.77 us (11%)
  between operations  0.99 us (1%)
  other arithmetic  0.78 us (1%)
    ppermute x28, starting transfers between devices, swap(): x = lax.ppermute(x, 'batch', [(i, i ^ bit) for i in every])  36.3 us
    ppermute x28, waiting for transfers between devices, swap(): x = lax.ppermute(x, 'batch', [(i, i ^ bit) for i in every])  27.8 us
    pallas_call x2, Pallas kernels, pack_tiles(): pl.pallas_call(kernel, out_shape=jax.ShapeDtypeStruct((len(offsets), heig...  3.22 us
    pallas_call x3, Pallas kernels, unpack_tiles(): pl.pallas_call(kernel, out_shape=[jax.ShapeDtypeStruct(shapes[p], kind) f...  3.1 us
  transfers between devices with their start and end apart: 28, of which 9 were waited for; matrix products, arithmetic and copies ran while one was open for 1% of the time, Pallas kernels for 7%

profile of v1, /device:TPU:0, one launch (start us, length us, event | category | flops | bytes accessed | tf_op | source)
XLA Modules:
  0.0 73.6 jit_solution(10792011832630891869)
XLA Ops:
  0.6 1.5 %shard_map.212 = f32[3,528,256]{2,1,0:T(8,128)S(1)} custom-call(f32[1024,256]{1,0:T(8,128)} %bitcast.85, f32[1024,256]{1,0:T(8,128)} %bitcast.87, f32[1024,256]{1,0:T(8,128)} %bitcast.89, f32[256,1024]{1,0:T(8,128)} %bitcast.91, f32[1,1024]{1,0:T(1,128)} %n.3, f32[1,1024]{1,0:T(1,128)} %b.3), custom_call_target="tpu_custom_call" | custom-call | tf_op jit(solution)/shard_map/pallas_call | solution.py:96
  2.2 3.0 %collective-permute-start.1 = (f16[272,256]{1,0:T(8,128)(2,1)S(1)}, f16[272,256]{1,0:T(8,128)(2,1)S(1)}, u32[]{:S(2)}, u32[]{:S(2)}) collective-permute-start(f16[272,256]{1,0:T(8,128)(2,1)S(1)} %get-tuple-element.64), channel_id=1, source_target_pairs={{0,4},{4,0},{8,12},{12,8},{16,20},{20,16},{24,28},{28,24},{1,5},{5... | collective-permute-start | bytes 417800 | tf_op jit(solution)/shard_map/ppermute | solution.py:295
  5.2 1.6 %collective-permute-start.5 = (f16[272,256]{1,0:T(8,128)(2,1)S(1)}, f16[272,256]{1,0:T(8,128)(2,1)S(1)}, u32[]{:S(2)}, u32[]{:S(2)}) collective-permute-start(f16[272,256]{1,0:T(8,128)(2,1)S(1)} %get-tuple-element.65), channel_id=1, source_target_pairs={{0,8},{4,12},{8,0},{12,4},{16,24},{20,28},{24,16},{28,20},{1,9},{5... | collective-permute-start | bytes 417800 | tf_op jit(solution)/shard_map/ppermute | solution.py:295
  7.5 1.5 %collective-permute-start.6 = (f16[256,256]{1,0:T(8,128)(2,1)S(1)}, f16[256,256]{1,0:T(8,128)(2,1)S(1)}, u32[]{:S(2)}, u32[]{:S(2)}) collective-permute-start(f16[256,256]{1,0:T(8,128)(2,1)S(1)} %get-tuple-element.67), channel_id=1, source_target_pairs={{0,4},{4,0},{8,12},{12,8},{16,20},{20,16},{24,28},{28,24},{1,5},{5... | collective-permute-start | bytes 393224 | tf_op jit(solution)/shard_map/ppermute | solution.py:295
  9.5 1.8 %shard_map.211 = f32[5,528,256]{2,1,0:T(8,128)S(1)} custom-call(f32[1024,256]{1,0:T(8,128)} %bitcast.86, f32[1024,256]{1,0:T(8,128)} %bitcast.88, f32[1024,256]{1,0:T(8,128)} %bitcast.90, f32[256,1024]{1,0:T(8,128)} %bitcast.92, f32[1,1024]{1,0:T(1,128)} %n.3, f32[1,1024]{1,0:T(1,128)} %b.3), custom_call_target="tpu_custom_call" | custom-call | tf_op jit(solution)/shard_map/pallas_call | solution.py:96
  11.5 4.4 %collective-permute-done.6 = f16[256,256]{1,0:T(8,128)(2,1)S(1)} collective-permute-done((f16[256,256]{1,0:T(8,128)(2,1)S(1)}, f16[256,256]{1,0:T(8,128)(2,1)S(1)}, u32[]{:S(2)}, u32[]{:S(2)}) %collective-permute-start.6) | collective-permute-done | bytes 131104 | tf_op jit(solution)/shard_map/ppermute | solution.py:295
  15.9 1.5 %collective-permute-start = (f16[256,256]{1,0:T(8,128)(2,1)S(1)}, f16[256,256]{1,0:T(8,128)(2,1)S(1)}, u32[]{:S(2)}, u32[]{:S(2)}) collective-permute-start(f16[256,256]{1,0:T(8,128)(2,1)S(1)} %fusion.40), channel_id=1, source_target_pairs={{0,4},{4,0},{8,12},{12,8},{16,20},{20,16},{24,28},{28,24},{1,5},{5... | collective-permute-start | bytes 393224 | tf_op jit(solution)/shard_map/ppermute | solution.py:295
  17.5 1.6 %collective-permute-start.7 = (f16[256,256]{1,0:T(8,128)(2,1)S(1)}, f16[256,256]{1,0:T(8,128)(2,1)S(1)}, u32[]{:S(2)}, u32[]{:S(2)}) collective-permute-start(f16[256,256]{1,0:T(8,128)(2,1)S(1)} %fusion.21), channel_id=1, source_target_pairs={{0,8},{4,12},{8,0},{12,4},{16,24},{20,28},{24,16},{28,20},{1,9},{5... | collective-permute-start | bytes 393224 | tf_op jit(solution)/shard_map/ppermute | solution.py:295
  19.8 3.7 %collective-permute-done.7 = f16[256,256]{1,0:T(8,128)(2,1)S(1)} collective-permute-done((f16[256,256]{1,0:T(8,128)(2,1)S(1)}, f16[256,256]{1,0:T(8,128)(2,1)S(1)}, u32[]{:S(2)}, u32[]{:S(2)}) %collective-permute-start.7) | collective-permute-done | bytes 131104 | tf_op jit(solution)/shard_map/ppermute | solution.py:295
  23.5 1.6 %collective-permute-start.2 = (f16[272,256]{1,0:T(8,128)(2,1)S(1)}, f16[272,256]{1,0:T(8,128)(2,1)S(1)}, u32[]{:S(2)}, u32[]{:S(2)}) collective-permute-start(f16[272,256]{1,0:T(8,128)(2,1)S(1)} %get-tuple-element.63), channel_id=1, source_target_pairs={{0,8},{4,12},{8,0},{12,4},{16,24},{20,28},{24,16},{28,20},{1,9},{5... | collective-permute-start | bytes 417800 | tf_op jit(solution)/shard_map/ppermute | solution.py:295
  25.5 5.5 %collective-permute-done.2 = f16[272,256]{1,0:T(8,128)(2,1)S(1)} collective-permute-done((f16[272,256]{1,0:T(8,128)(2,1)S(1)}, f16[272,256]{1,0:T(8,128)(2,1)S(1)}, u32[]{:S(2)}, u32[]{:S(2)}) %collective-permute-start.2) | collective-permute-done | bytes 139296 | tf_op jit(solution)/shard_map/ppermute | solution.py:295
  31.4 3.9 %collective-permute-start.9 = (f16[256,256]{1,0:T(8,128)(2,1)S(1)}, f16[256,256]{1,0:T(8,128)(2,1)S(1)}, u32[]{:S(2)}, u32[]{:S(2)}) collective-permute-start(f16[256,256]{1,0:T(8,128)(2,1)S(1)} %fusion.26), channel_id=1, source_target_pairs={{0,16},{4,20},{8,24},{12,28},{16,0},{20,4},{24,8},{28,12},{1,17},{... | collective-permute-start | bytes 393224 | tf_op jit(solution)/shard_map/ppermute | solution.py:295
  36.2 3.9 %collective-permute-done.10 = f16[256,256]{1,0:T(8,128)(2,1)S(1)} collective-permute-done((f16[256,256]{1,0:T(8,128)(2,1)S(1)}, f16[256,256]{1,0:T(8,128)(2,1)S(1)}, u32[]{:S(2)}, u32[]{:S(2)}) %collective-permute-start.10) | collective-permute-done | bytes 131104 | tf_op jit(solution)/shard_map/ppermute | solution.py:295
  40.2 3.6 %collective-permute-done.9 = f16[256,256]{1,0:T(8,128)(2,1)S(1)} collective-permute-done((f16[256,256]{1,0:T(8,128)(2,1)S(1)}, f16[256,256]{1,0:T(8,128)(2,1)S(1)}, u32[]{:S(2)}, u32[]{:S(2)}) %collective-permute-start.9) | collective-permute-done | bytes 131104 | tf_op jit(solution)/shard_map/ppermute | solution.py:295
  44.7 2.5 %collective-permute-start.12 = (bf16[256,256]{1,0:T(8,128)(2,1)S(1)}, bf16[256,256]{1,0:T(8,128)(2,1)S(1)}, u32[]{:S(2)}, u32[]{:S(2)}) collective-permute-start(bf16[256,256]{1,0:T(8,128)(2,1)S(1)} %get-tuple-element.43.refs_0_), channel_id=1, source_target_pairs={{0,8},{4,12},{8,0},{12,4},{16,24},{20,28},{24,16},{28,20},{1,9},{5... | collective-permute-start | bytes 393224 | tf_op jit(solution)/shard_map/ppermute | solution.py:295
  48.1 5.0 %collective-permute-start.21 = (bf16[264,256]{1,0:T(8,128)(2,1)S(1)}, bf16[264,256]{1,0:T(8,128)(2,1)S(1)}, u32[]{:S(2)}, u32[]{:S(2)}) collective-permute-start(bf16[264,256]{1,0:T(8,128)(2,1)S(1)} %get-tuple-element.47.refs_0_), channel_id=1, source_target_pairs={{0,16},{4,20},{8,24},{12,28},{16,0},{20,4},{24,8},{28,12},{1,17},{... | collective-permute-start | bytes 405512 | tf_op jit(solution)/shard_map/ppermute | solution.py:295
  53.6 1.5 %collective-permute-start.15 = (bf16[256,256]{1,0:T(8,128)(2,1)S(1)}, bf16[256,256]{1,0:T(8,128)(2,1)S(1)}, u32[]{:S(2)}, u32[]{:S(2)}) collective-permute-start(bf16[256,256]{1,0:T(8,128)(2,1)S(1)} %collective-permute-done.14.refs_4_), channel_id=1, source_target_pairs={{0,4},{4,0},{8,12},{12,8},{16,20},{20,16},{24,28},{28,24},{1,5},{5... | collective-permute-start | bytes 393224 | tf_op jit(solution)/shard_map/ppermute | solution.py:295
  55.1 1.2 %collective-permute-done.21.refs_4_ = bf16[264,256]{1,0:T(8,128)(2,1)S(1)} collective-permute-done((bf16[264,256]{1,0:T(8,128)(2,1)S(1)}, bf16[264,256]{1,0:T(8,128)(2,1)S(1)}, u32[]{:S(2)}, u32[]{:S(2)}) %collective-permute-start.21) | collective-permute-done | bytes 135200 | tf_op jit(solution)/shard_map/ppermute | solution.py:295
  56.8 4.1 %collective-permute-start.22 = (bf16[264,256]{1,0:T(8,128)(2,1)S(1)}, bf16[264,256]{1,0:T(8,128)(2,1)S(1)}, u32[]{:S(2)}, u32[]{:S(2)}) collective-permute-start(bf16[264,256]{1,0:T(8,128)(2,1)S(1)} %collective-permute-done.21.refs_4_), channel_id=1, source_target_pairs={{0,8},{4,12},{8,0},{12,4},{16,24},{20,28},{24,16},{28,20},{1,9},{5... | collective-permute-start | bytes 405512 | tf_op jit(solution)/shard_map/ppermute | solution.py:295
  61.4 1.5 %collective-permute-start.11 = (bf16[256,256]{1,0:T(8,128)(2,1)S(1)}, bf16[256,256]{1,0:T(8,128)(2,1)S(1)}, u32[]{:S(2)}, u32[]{:S(2)}) collective-permute-start(bf16[256,256]{1,0:T(8,128)(2,1)S(1)} %get-tuple-element.43.refs_0_), channel_id=1, source_target_pairs={{0,4},{4,0},{8,12},{12,8},{16,20},{20,16},{24,28},{28,24},{1,5},{5... | collective-permute-start | bytes 393224 | tf_op jit(solution)/shard_map/ppermute | solution.py:295
  63.0 2.9 %collective-permute-done.26.refs_3_ = bf16[264,256]{1,0:T(8,128)(2,1)S(1)} collective-permute-done((bf16[264,256]{1,0:T(8,128)(2,1)S(1)}, bf16[264,256]{1,0:T(8,128)(2,1)S(1)}, u32[]{:S(2)}, u32[]{:S(2)}) %collective-permute-start.26) | collective-permute-done | bytes 135200 | tf_op jit(solution)/shard_map/ppermute | solution.py:295
  69.0 1.9 %collective-permute-done.13.refs_3_ = bf16[256,256]{1,0:T(8,128)(2,1)S(1)} collective-permute-done((bf16[256,256]{1,0:T(8,128)(2,1)S(1)}, bf16[256,256]{1,0:T(8,128)(2,1)S(1)}, u32[]{:S(2)}, u32[]{:S(2)}) %collective-permute-start.13) | collective-permute-done | bytes 131104 | tf_op jit(solution)/shard_map/ppermute | solution.py:295
  71.4 1.0 %unpack.3 = (bf16[1024,256]{1,0:T(8,128)(2,1)}, bf16[1024,256]{1,0:T(8,128)(2,1)}) custom-call(bf16[256,256]{1,0:T(8,128)(2,1)S(1)} %get-tuple-element.43.refs_0_, bf16[256,256]{1,0:T(8,128)(2,1)S(1)} %collective-permute-done.11.refs_1_, bf16[256,256]{1,0:T(8,128)(2,1)S(1)} %collective-permute-done.12.refs_2_, ...), custom_call_target="tpu_custom_call" | custom-call | tf_op jit(solution)/shard_map/unpack/pallas_call | solution.py:204
  72.4 1.2 %unpack.5 = (bf16[1024,256]{1,0:T(8,128)(2,1)}, bf16[256,1024]{1,0:T(8,128)(2,1)}, bf16[8,128]{1,0:T(8,128)(2,1)}, bf16[8,128]{1,0:T(8,128)(2,1)}) custom-call(bf16[264,256]{1,0:T(8,128)(2,1)S(1)} %collective-permute-done.23.refs_0_, f32[1,128]{1,0:T(1,128)S(1)} %broadcast_add_fusion.refs_8_.refs_7_.refs_1_, ...), custom_call_target="tpu_custom_call", output_to_operand_aliasing={{0}: (2, {}), {1}: (3, {})} | custom-call | tf_op jit(solution)/shard_map/unpack/pallas_call | solution.py:204
  (77 shorter events, 10.7 us)
Async XLA Ops:
  2.2 33.2 %collective-permute-start.1 = (f16[272,256]{1,0:T(8,128)(2,1)S(1)}, f16[272,256]{1,0:T(8,128)(2,1)S(1)}, u32[]{:S(2)}, u32[]{:S(2)}) collective-permute-start(f16[272,256]{1,0:T(8,128)(2,1)S(1)} %get-tuple-element.64), channel_id=1, source_target_pairs={{0,4},{4,0},{8,12},{12,8},{16,20},{20,16},{24,28},{28,24},{1,5},{5... | collective-permute-start | bytes 417800 | tf_op jit(solution)/shard_map/ppermute | solution.py:295
  5.2 12.2 %collective-permute-start.5 = (f16[272,256]{1,0:T(8,128)(2,1)S(1)}, f16[272,256]{1,0:T(8,128)(2,1)S(1)}, u32[]{:S(2)}, u32[]{:S(2)}) collective-permute-start(f16[272,256]{1,0:T(8,128)(2,1)S(1)} %get-tuple-element.65), channel_id=1, source_target_pairs={{0,8},{4,12},{8,0},{12,4},{16,24},{20,28},{24,16},{28,20},{1,9},{5... | collective-permute-start | bytes 417800 | tf_op jit(solution)/shard_map/ppermute | solution.py:295
  6.9 12.3 %collective-permute-start.4 = (f16[256,256]{1,0:T(8,128)(2,1)S(1)}, f16[256,256]{1,0:T(8,128)(2,1)S(1)}, u32[]{:S(2)}, u32[]{:S(2)}) collective-permute-start(f16[256,256]{1,0:T(8,128)(2,1)S(1)} %get-tuple-element.66), channel_id=1, source_target_pairs={{0,4},{4,0},{8,12},{12,8},{16,20},{20,16},{24,28},{28,24},{1,5},{5... | collective-permute-start | bytes 393224 | tf_op jit(solution)/shard_map/ppermute | solution.py:295
  7.5 8.4 %collective-permute-start.6 = (f16[256,256]{1,0:T(8,128)(2,1)S(1)}, f16[256,256]{1,0:T(8,128)(2,1)S(1)}, u32[]{:S(2)}, u32[]{:S(2)}) collective-permute-start(f16[256,256]{1,0:T(8,128)(2,1)S(1)} %get-tuple-element.67), channel_id=1, source_target_pairs={{0,4},{4,0},{8,12},{12,8},{16,20},{20,16},{24,28},{28,24},{1,5},{5... | collective-permute-start | bytes 393224 | tf_op jit(solution)/shard_map/ppermute | solution.py:295
  9.0 16.2 %collective-permute-start.3 = (f16[256,256]{1,0:T(8,128)(2,1)S(1)}, f16[256,256]{1,0:T(8,128)(2,1)S(1)}, u32[]{:S(2)}, u32[]{:S(2)}) collective-permute-start(f16[256,256]{1,0:T(8,128)(2,1)S(1)} %get-tuple-element.68), channel_id=1, source_target_pairs={{0,4},{4,0},{8,12},{12,8},{16,20},{20,16},{24,28},{28,24},{1,5},{5... | collective-permute-start | bytes 393224 | tf_op jit(solution)/shard_map/ppermute | solution.py:295
  15.9 19.6 %collective-permute-start = (f16[256,256]{1,0:T(8,128)(2,1)S(1)}, f16[256,256]{1,0:T(8,128)(2,1)S(1)}, u32[]{:S(2)}, u32[]{:S(2)}) collective-permute-start(f16[256,256]{1,0:T(8,128)(2,1)S(1)} %fusion.40), channel_id=1, source_target_pairs={{0,4},{4,0},{8,12},{12,8},{16,20},{20,16},{24,28},{28,24},{1,5},{5... | collective-permute-start | bytes 393224 | tf_op jit(solution)/shard_map/ppermute | solution.py:295
  17.5 6.0 %collective-permute-start.7 = (f16[256,256]{1,0:T(8,128)(2,1)S(1)}, f16[256,256]{1,0:T(8,128)(2,1)S(1)}, u32[]{:S(2)}, u32[]{:S(2)}) collective-permute-start(f16[256,256]{1,0:T(8,128)(2,1)S(1)} %fusion.21), channel_id=1, source_target_pairs={{0,8},{4,12},{8,0},{12,4},{16,24},{20,28},{24,16},{28,20},{1,9},{5... | collective-permute-start | bytes 393224 | tf_op jit(solution)/shard_map/ppermute | solution.py:295
  19.2 28.1 %collective-permute-start.20 = (f16[272,256]{1,0:T(8,128)(2,1)S(1)}, f16[272,256]{1,0:T(8,128)(2,1)S(1)}, u32[]{:S(2)}, u32[]{:S(2)}) collective-permute-start(f16[272,256]{1,0:T(8,128)(2,1)S(1)} %get-tuple-element.62), channel_id=1, source_target_pairs={{0,4},{4,0},{8,12},{12,8},{16,20},{20,16},{24,28},{28,24},{1,5},{5... | collective-permute-start | bytes 417800 | tf_op jit(solution)/shard_map/ppermute | solution.py:295
  23.5 7.5 %collective-permute-start.2 = (f16[272,256]{1,0:T(8,128)(2,1)S(1)}, f16[272,256]{1,0:T(8,128)(2,1)S(1)}, u32[]{:S(2)}, u32[]{:S(2)}) collective-permute-start(f16[272,256]{1,0:T(8,128)(2,1)S(1)} %get-tuple-element.63), channel_id=1, source_target_pairs={{0,8},{4,12},{8,0},{12,4},{16,24},{20,28},{24,16},{28,20},{1,9},{5... | collective-permute-start | bytes 417800 | tf_op jit(solution)/shard_map/ppermute | solution.py:295
  25.1 6.3 %collective-permute-start.8 = (f16[272,256]{1,0:T(8,128)(2,1)S(1)}, f16[272,256]{1,0:T(8,128)(2,1)S(1)}, u32[]{:S(2)}, u32[]{:S(2)}) collective-permute-start(f16[272,256]{1,0:T(8,128)(2,1)S(1)} %fusion.8), channel_id=1, source_target_pairs={{0,4},{4,0},{8,12},{12,8},{16,20},{20,16},{24,28},{28,24},{1,5},{5... | collective-permute-start | bytes 417800 | tf_op jit(solution)/shard_map/ppermute | solution.py:295
  31.0 9.2 %collective-permute-start.10 = (f16[256,256]{1,0:T(8,128)(2,1)S(1)}, f16[256,256]{1,0:T(8,128)(2,1)S(1)}, u32[]{:S(2)}, u32[]{:S(2)}) collective-permute-start(f16[256,256]{1,0:T(8,128)(2,1)S(1)} %fusion.30), channel_id=1, source_target_pairs={{0,8},{4,12},{8,0},{12,4},{16,24},{20,28},{24,16},{28,20},{1,9},{5... | collective-permute-start | bytes 393224 | tf_op jit(solution)/shard_map/ppermute | solution.py:295
  31.4 12.4 %collective-permute-start.9 = (f16[256,256]{1,0:T(8,128)(2,1)S(1)}, f16[256,256]{1,0:T(8,128)(2,1)S(1)}, u32[]{:S(2)}, u32[]{:S(2)}) collective-permute-start(f16[256,256]{1,0:T(8,128)(2,1)S(1)} %fusion.26), channel_id=1, source_target_pairs={{0,16},{4,20},{8,24},{12,28},{16,0},{20,4},{24,8},{28,12},{1,17},{... | collective-permute-start | bytes 393224 | tf_op jit(solution)/shard_map/ppermute | solution.py:295
  35.4 11.8 %collective-permute-start.18 = (f16[272,256]{1,0:T(8,128)(2,1)S(1)}, f16[272,256]{1,0:T(8,128)(2,1)S(1)}, u32[]{:S(2)}, u32[]{:S(2)}) collective-permute-start(f16[272,256]{1,0:T(8,128)(2,1)S(1)} %fusion.13), channel_id=1, source_target_pairs={{0,16},{4,20},{8,24},{12,28},{16,0},{20,4},{24,8},{28,12},{1,17},{... | collective-permute-start | bytes 417800 | tf_op jit(solution)/shard_map/ppermute | solution.py:295
  35.5 11.7 %collective-permute-start.19 = (f16[272,256]{1,0:T(8,128)(2,1)S(1)}, f16[272,256]{1,0:T(8,128)(2,1)S(1)}, u32[]{:S(2)}, u32[]{:S(2)}) collective-permute-start(f16[272,256]{1,0:T(8,128)(2,1)S(1)} %fusion.17), channel_id=1, source_target_pairs={{0,8},{4,12},{8,0},{12,4},{16,24},{20,28},{24,16},{28,20},{1,9},{5... | collective-permute-start | bytes 417800 | tf_op jit(solution)/shard_map/ppermute | solution.py:295
  44.7 9.0 %collective-permute-start.14 = (bf16[256,256]{1,0:T(8,128)(2,1)S(1)}, bf16[256,256]{1,0:T(8,128)(2,1)S(1)}, u32[]{:S(2)}, u32[]{:S(2)}) collective-permute-start(bf16[256,256]{1,0:T(8,128)(2,1)S(1)} %get-tuple-element.43.refs_0_), channel_id=1, source_target_pairs={{0,16},{4,20},{8,24},{12,28},{16,0},{20,4},{24,8},{28,12},{1,17},{... | collective-permute-start | bytes 393224 | tf_op jit(solution)/shard_map/ppermute | solution.py:295
  44.7 12.2 %collective-permute-start.12 = (bf16[256,256]{1,0:T(8,128)(2,1)S(1)}, bf16[256,256]{1,0:T(8,128)(2,1)S(1)}, u32[]{:S(2)}, u32[]{:S(2)}) collective-permute-start(bf16[256,256]{1,0:T(8,128)(2,1)S(1)} %get-tuple-element.43.refs_0_), channel_id=1, source_target_pairs={{0,8},{4,12},{8,0},{12,4},{16,24},{20,28},{24,16},{28,20},{1,9},{5... | collective-permute-start | bytes 393224 | tf_op jit(solution)/shard_map/ppermute | solution.py:295
  48.1 12.9 %collective-permute-start.25 = (bf16[264,256]{1,0:T(8,128)(2,1)S(1)}, bf16[264,256]{1,0:T(8,128)(2,1)S(1)}, u32[]{:S(2)}, u32[]{:S(2)}) collective-permute-start(bf16[264,256]{1,0:T(8,128)(2,1)S(1)} %get-tuple-element.47.refs_0_), channel_id=1, source_target_pairs={{0,8},{4,12},{8,0},{12,4},{16,24},{20,28},{24,16},{28,20},{1,9},{5... | collective-permute-start | bytes 405512 | tf_op jit(solution)/shard_map/ppermute | solution.py:295
  48.1 8.3 %collective-permute-start.21 = (bf16[264,256]{1,0:T(8,128)(2,1)S(1)}, bf16[264,256]{1,0:T(8,128)(2,1)S(1)}, u32[]{:S(2)}, u32[]{:S(2)}) collective-permute-start(bf16[264,256]{1,0:T(8,128)(2,1)S(1)} %get-tuple-element.47.refs_0_), channel_id=1, source_target_pairs={{0,16},{4,20},{8,24},{12,28},{16,0},{20,4},{24,8},{28,12},{1,17},{... | collective-permute-start | bytes 405512 | tf_op jit(solution)/shard_map/ppermute | solution.py:295
  53.1 8.3 %collective-permute-start.24 = (bf16[264,256]{1,0:T(8,128)(2,1)S(1)}, bf16[264,256]{1,0:T(8,128)(2,1)S(1)}, u32[]{:S(2)}, u32[]{:S(2)}) collective-permute-start(bf16[264,256]{1,0:T(8,128)(2,1)S(1)} %get-tuple-element.47.refs_0_), channel_id=1, source_target_pairs={{0,4},{4,0},{8,12},{12,8},{16,20},{20,16},{24,28},{28,24},{1,5},{5... | collective-permute-start | bytes 405512 | tf_op jit(solution)/shard_map/ppermute | solution.py:295
  53.6 9.3 %collective-permute-start.15 = (bf16[256,256]{1,0:T(8,128)(2,1)S(1)}, bf16[256,256]{1,0:T(8,128)(2,1)S(1)}, u32[]{:S(2)}, u32[]{:S(2)}) collective-permute-start(bf16[256,256]{1,0:T(8,128)(2,1)S(1)} %collective-permute-done.14.refs_4_), channel_id=1, source_target_pairs={{0,4},{4,0},{8,12},{12,8},{16,20},{20,16},{24,28},{28,24},{1,5},{5... | collective-permute-start | bytes 393224 | tf_op jit(solution)/shard_map/ppermute | solution.py:295
  56.3 10.1 %collective-permute-start.27 = (bf16[264,256]{1,0:T(8,128)(2,1)S(1)}, bf16[264,256]{1,0:T(8,128)(2,1)S(1)}, u32[]{:S(2)}, u32[]{:S(2)}) collective-permute-start(bf16[264,256]{1,0:T(8,128)(2,1)S(1)} %collective-permute-done.21.refs_4_), channel_id=1, source_target_pairs={{0,4},{4,0},{8,12},{12,8},{16,20},{20,16},{24,28},{28,24},{1,5},{5... | collective-permute-start | bytes 405512 | tf_op jit(solution)/shard_map/ppermute | solution.py:295
  56.8 10.5 %collective-permute-start.22 = (bf16[264,256]{1,0:T(8,128)(2,1)S(1)}, bf16[264,256]{1,0:T(8,128)(2,1)S(1)}, u32[]{:S(2)}, u32[]{:S(2)}) collective-permute-start(bf16[264,256]{1,0:T(8,128)(2,1)S(1)} %collective-permute-done.21.refs_4_), channel_id=1, source_target_pairs={{0,8},{4,12},{8,0},{12,4},{16,24},{20,28},{24,16},{28,20},{1,9},{5... | collective-permute-start | bytes 405512 | tf_op jit(solution)/shard_map/ppermute | solution.py:295
  61.4 7.5 %collective-permute-start.11 = (bf16[256,256]{1,0:T(8,128)(2,1)S(1)}, bf16[256,256]{1,0:T(8,128)(2,1)S(1)}, u32[]{:S(2)}, u32[]{:S(2)}) collective-permute-start(bf16[256,256]{1,0:T(8,128)(2,1)S(1)} %get-tuple-element.43.refs_0_), channel_id=1, source_target_pairs={{0,4},{4,0},{8,12},{12,8},{16,20},{20,16},{24,28},{28,24},{1,5},{5... | collective-permute-start | bytes 393224 | tf_op jit(solution)/shard_map/ppermute | solution.py:295
  63.0 6.0 %collective-permute-start.16 = (bf16[256,256]{1,0:T(8,128)(2,1)S(1)}, bf16[256,256]{1,0:T(8,128)(2,1)S(1)}, u32[]{:S(2)}, u32[]{:S(2)}) collective-permute-start(bf16[256,256]{1,0:T(8,128)(2,1)S(1)} %collective-permute-done.14.refs_4_), channel_id=1, source_target_pairs={{0,8},{4,12},{8,0},{12,4},{16,24},{20,28},{24,16},{28,20},{1,9},{5... | collective-permute-start | bytes 393224 | tf_op jit(solution)/shard_map/ppermute | solution.py:295
  (10 other events, 177.0 us)

commit v2 on v1

--- a/solution.py
+++ b/solution.py
@@ -228,8 +228,8 @@
 order_of_8 = (
     ((0, 7, 0),), ((0, 5, 0),), ((0, 7, 1),), ((0, 3, 0),), ((0, 6, 0),), ((0, 6, 1),), ((0, 5, 1),),
     ((0, 3, 1),), ((0, 1, 0),), ((0, 4, 0),), ((0, 2, 0),), ((0, 4, 1),), ((0, 2, 1),), ((0, 1, 1),),
-    ((1, 4, 0),), ((1, 1, 0),), ((1, 2, 0),), ((1, 1, 1),), ((1, 4, 1),), ((1, 2, 1),), ((1, 3, 0),),
-    ((1, 5, 0),), ((1, 5, 1),), ((1, 6, 1),), ((1, 6, 0),), ((1, 3, 1),), ((1, 7, 0),), ((1, 7, 1),),
+    ((1, 4, 0),), ((1, 2, 0),), ((1, 1, 0),), ((1, 1, 1),), ((1, 4, 1),), ((1, 3, 0),), ((1, 2, 1),),
+    ((1, 5, 0),), ((1, 6, 1),), ((1, 5, 1),), ((1, 6, 0),), ((1, 3, 1),), ((1, 7, 0),), ((1, 7, 1),),
 )
 bits_of_8 = {(0, 7, 1): 2, (1, 7, 0): 2}
 packs_of_8 = ((7, 5, 3), (6, 1, 4, 2, 0))
@@ -345,7 +345,8 @@
         if not fits:
             done = unpack_plain([mine[j] for j in range(replicas)], rows, cols, replicas)
         elif g == order[-1][-1][2]:
-            last = {at[1]: mine.pop(at[1]) for at in order[-1]}
+            last = [at[1] for exchange in order for at in exchange if at[0] == 1 and at[2] == g][-2:]
+            last = {j: mine.pop(j) for j in last}
             done = unpack_tiles(mine, [], tick, parts, rows, cols, replicas)
             done = unpack_tiles(last, done, tick, parts, rows, cols, replicas)
         else:

time: 73.8 us -> 70.1 us (0.950)
  waiting for transfers between devices: 27.8 us -> 24.2 us
    ppermute x28, waiting for transfers between devices: 27.8 us -> 24.2 us  [swap(): x = lax.ppermute(x, 'batch', [(i, i ^ bit) for i in every])]
  transfers between devices with their start and end apart: 28 -> 28, of which waited for: 9 -> 10; matrix products, arithmetic and copies ran while one was open for 1% -> 1% of each run, Pallas kernels for 7% -> 7%
where the time goes in v2:
time: 70.1 us; the launch traced here: 69.9 us
  starting transfers between devices  36.1 us (51%)
  waiting for transfers between devices  24.2 us (35%)
  Pallas kernels  7.78 us (11%)
  between operations  0.99 us (1%)
  other arithmetic  0.78 us (1%)
    ppermute x28, starting transfers between devices, swap(): x = lax.ppermute(x, 'batch', [(i, i ^ bit) for i in every])  36.1 us
    ppermute x28, waiting for transfers between devices, swap(): x = lax.ppermute(x, 'batch', [(i, i ^ bit) for i in every])  24.2 us
    pallas_call x2, Pallas kernels, pack_tiles(): pl.pallas_call(kernel, out_shape=jax.ShapeDtypeStruct((len(offsets), heig...  3.22 us
    pallas_call x3, Pallas kernels, unpack_tiles(): pl.pallas_call(kernel, out_shape=[jax.ShapeDtypeStruct(shapes[p], kind) f...  3.11 us
    pallas_call x2, Pallas kernels, step_tiles(): pl.pallas_call(kernel, out_shape=[jax.ShapeDtypeStruct((height + tail, co...  1.45 us
  transfers between devices with their start and end apart: 28, of which 10 were waited for; matrix products, arithmetic and copies ran while one was open for 1% of the time, Pallas kernels for 7%

profile of v2, /device:TPU:0, one launch (start us, length us, event | category | flops | bytes accessed | tf_op | source)
XLA Modules:
  0.0 69.9 jit_solution(12103036305632198101)
XLA Ops:
  0.6 1.5 %shard_map.212 = f32[3,528,256]{2,1,0:T(8,128)S(1)} custom-call(f32[1024,256]{1,0:T(8,128)} %bitcast.85, f32[1024,256]{1,0:T(8,128)} %bitcast.87, f32[1024,256]{1,0:T(8,128)} %bitcast.89, f32[256,1024]{1,0:T(8,128)} %bitcast.91, f32[1,1024]{1,0:T(1,128)} %n.3, f32[1,1024]{1,0:T(1,128)} %b.3), custom_call_target="tpu_custom_call" | custom-call | tf_op jit(solution)/shard_map/pallas_call | solution.py:96
  2.2 3.0 %collective-permute-start.1 = (f16[272,256]{1,0:T(8,128)(2,1)S(1)}, f16[272,256]{1,0:T(8,128)(2,1)S(1)}, u32[]{:S(2)}, u32[]{:S(2)}) collective-permute-start(f16[272,256]{1,0:T(8,128)(2,1)S(1)} %get-tuple-element.64), channel_id=1, source_target_pairs={{0,4},{4,0},{8,12},{12,8},{16,20},{20,16},{24,28},{28,24},{1,5},{5... | collective-permute-start | bytes 417800 | tf_op jit(solution)/shard_map/ppermute | solution.py:295
  5.2 1.6 %collective-permute-start.5 = (f16[272,256]{1,0:T(8,128)(2,1)S(1)}, f16[272,256]{1,0:T(8,128)(2,1)S(1)}, u32[]{:S(2)}, u32[]{:S(2)}) collective-permute-start(f16[272,256]{1,0:T(8,128)(2,1)S(1)} %get-tuple-element.65), channel_id=1, source_target_pairs={{0,8},{4,12},{8,0},{12,4},{16,24},{20,28},{24,16},{28,20},{1,9},{5... | collective-permute-start | bytes 417800 | tf_op jit(solution)/shard_map/ppermute | solution.py:295
  7.5 1.5 %collective-permute-start.6 = (f16[256,256]{1,0:T(8,128)(2,1)S(1)}, f16[256,256]{1,0:T(8,128)(2,1)S(1)}, u32[]{:S(2)}, u32[]{:S(2)}) collective-permute-start(f16[256,256]{1,0:T(8,128)(2,1)S(1)} %get-tuple-element.67), channel_id=1, source_target_pairs={{0,4},{4,0},{8,12},{12,8},{16,20},{20,16},{24,28},{28,24},{1,5},{5... | collective-permute-start | bytes 393224 | tf_op jit(solution)/shard_map/ppermute | solution.py:295
  9.5 1.8 %shard_map.211 = f32[5,528,256]{2,1,0:T(8,128)S(1)} custom-call(f32[1024,256]{1,0:T(8,128)} %bitcast.86, f32[1024,256]{1,0:T(8,128)} %bitcast.88, f32[1024,256]{1,0:T(8,128)} %bitcast.90, f32[256,1024]{1,0:T(8,128)} %bitcast.92, f32[1,1024]{1,0:T(1,128)} %n.3, f32[1,1024]{1,0:T(1,128)} %b.3), custom_call_target="tpu_custom_call" | custom-call | tf_op jit(solution)/shard_map/pallas_call | solution.py:96
  11.5 4.4 %collective-permute-done.6 = f16[256,256]{1,0:T(8,128)(2,1)S(1)} collective-permute-done((f16[256,256]{1,0:T(8,128)(2,1)S(1)}, f16[256,256]{1,0:T(8,128)(2,1)S(1)}, u32[]{:S(2)}, u32[]{:S(2)}) %collective-permute-start.6) | collective-permute-done | bytes 131104 | tf_op jit(solution)/shard_map/ppermute | solution.py:295
  15.9 1.5 %collective-permute-start = (f16[256,256]{1,0:T(8,128)(2,1)S(1)}, f16[256,256]{1,0:T(8,128)(2,1)S(1)}, u32[]{:S(2)}, u32[]{:S(2)}) collective-permute-start(f16[256,256]{1,0:T(8,128)(2,1)S(1)} %fusion.40), channel_id=1, source_target_pairs={{0,4},{4,0},{8,12},{12,8},{16,20},{20,16},{24,28},{28,24},{1,5},{5... | collective-permute-start | bytes 393224 | tf_op jit(solution)/shard_map/ppermute | solution.py:295
  17.5 1.6 %collective-permute-start.7 = (f16[256,256]{1,0:T(8,128)(2,1)S(1)}, f16[256,256]{1,0:T(8,128)(2,1)S(1)}, u32[]{:S(2)}, u32[]{:S(2)}) collective-permute-start(f16[256,256]{1,0:T(8,128)(2,1)S(1)} %fusion.21), channel_id=1, source_target_pairs={{0,8},{4,12},{8,0},{12,4},{16,24},{20,28},{24,16},{28,20},{1,9},{5... | collective-permute-start | bytes 393224 | tf_op jit(solution)/shard_map/ppermute | solution.py:295
  19.8 3.7 %collective-permute-done.7 = f16[256,256]{1,0:T(8,128)(2,1)S(1)} collective-permute-done((f16[256,256]{1,0:T(8,128)(2,1)S(1)}, f16[256,256]{1,0:T(8,128)(2,1)S(1)}, u32[]{:S(2)}, u32[]{:S(2)}) %collective-permute-start.7) | collective-permute-done | bytes 131104 | tf_op jit(solution)/shard_map/ppermute | solution.py:295
  23.5 1.6 %collective-permute-start.2 = (f16[272,256]{1,0:T(8,128)(2,1)S(1)}, f16[272,256]{1,0:T(8,128)(2,1)S(1)}, u32[]{:S(2)}, u32[]{:S(2)}) collective-permute-start(f16[272,256]{1,0:T(8,128)(2,1)S(1)} %get-tuple-element.63), channel_id=1, source_target_pairs={{0,8},{4,12},{8,0},{12,4},{16,24},{20,28},{24,16},{28,20},{1,9},{5... | collective-permute-start | bytes 417800 | tf_op jit(solution)/shard_map/ppermute | solution.py:295
  25.5 5.5 %collective-permute-done.2 = f16[272,256]{1,0:T(8,128)(2,1)S(1)} collective-permute-done((f16[272,256]{1,0:T(8,128)(2,1)S(1)}, f16[272,256]{1,0:T(8,128)(2,1)S(1)}, u32[]{:S(2)}, u32[]{:S(2)}) %collective-permute-start.2) | collective-permute-done | bytes 139296 | tf_op jit(solution)/shard_map/ppermute | solution.py:295
  31.4 3.9 %collective-permute-start.9 = (f16[256,256]{1,0:T(8,128)(2,1)S(1)}, f16[256,256]{1,0:T(8,128)(2,1)S(1)}, u32[]{:S(2)}, u32[]{:S(2)}) collective-permute-start(f16[256,256]{1,0:T(8,128)(2,1)S(1)} %fusion.26), channel_id=1, source_target_pairs={{0,16},{4,20},{8,24},{12,28},{16,0},{20,4},{24,8},{28,12},{1,17},{... | collective-permute-start | bytes 393224 | tf_op jit(solution)/shard_map/ppermute | solution.py:295
  36.2 3.9 %collective-permute-done.10 = f16[256,256]{1,0:T(8,128)(2,1)S(1)} collective-permute-done((f16[256,256]{1,0:T(8,128)(2,1)S(1)}, f16[256,256]{1,0:T(8,128)(2,1)S(1)}, u32[]{:S(2)}, u32[]{:S(2)}) %collective-permute-start.10) | collective-permute-done | bytes 131104 | tf_op jit(solution)/shard_map/ppermute | solution.py:295
  40.2 2.9 %collective-permute-done.9 = f16[256,256]{1,0:T(8,128)(2,1)S(1)} collective-permute-done((f16[256,256]{1,0:T(8,128)(2,1)S(1)}, f16[256,256]{1,0:T(8,128)(2,1)S(1)}, u32[]{:S(2)}, u32[]{:S(2)}) %collective-permute-start.9) | collective-permute-done | bytes 131104 | tf_op jit(solution)/shard_map/ppermute | solution.py:295
  44.0 4.5 %collective-permute-start.12 = (bf16[256,256]{1,0:T(8,128)(2,1)S(1)}, bf16[256,256]{1,0:T(8,128)(2,1)S(1)}, u32[]{:S(2)}, u32[]{:S(2)}) collective-permute-start(bf16[256,256]{1,0:T(8,128)(2,1)S(1)} %get-tuple-element.43.refs_0_), channel_id=1, source_target_pairs={{0,8},{4,12},{8,0},{12,4},{16,24},{20,28},{24,16},{28,20},{1,9},{5... | collective-permute-start | bytes 393224 | tf_op jit(solution)/shard_map/ppermute | solution.py:295
  49.3 2.1 %collective-permute-start.26 = (bf16[264,256]{1,0:T(8,128)(2,1)S(1)}, bf16[264,256]{1,0:T(8,128)(2,1)S(1)}, u32[]{:S(2)}, u32[]{:S(2)}) collective-permute-start(bf16[264,256]{1,0:T(8,128)(2,1)S(1)} %get-tuple-element.47.refs_0_), channel_id=1, source_target_pairs={{0,4},{4,0},{8,12},{12,8},{16,20},{20,16},{24,28},{28,24},{1,5},{5... | collective-permute-start | bytes 405512 | tf_op jit(solution)/shard_map/ppermute | solution.py:295
  51.4 3.0 %collective-permute-start.21 = (bf16[264,256]{1,0:T(8,128)(2,1)S(1)}, bf16[264,256]{1,0:T(8,128)(2,1)S(1)}, u32[]{:S(2)}, u32[]{:S(2)}) collective-permute-start(bf16[264,256]{1,0:T(8,128)(2,1)S(1)} %get-tuple-element.47.refs_0_), channel_id=1, source_target_pairs={{0,8},{4,12},{8,0},{12,4},{16,24},{20,28},{24,16},{28,20},{1,9},{5... | collective-permute-start | bytes 405512 | tf_op jit(solution)/shard_map/ppermute | solution.py:295
  54.4 1.2 %collective-permute-start.15 = (bf16[256,256]{1,0:T(8,128)(2,1)S(1)}, bf16[256,256]{1,0:T(8,128)(2,1)S(1)}, u32[]{:S(2)}, u32[]{:S(2)}) collective-permute-start(bf16[256,256]{1,0:T(8,128)(2,1)S(1)} %collective-permute-done.14.refs_4_), channel_id=1, source_target_pairs={{0,4},{4,0},{8,12},{12,8},{16,20},{20,16},{24,28},{28,24},{1,5},{5... | collective-permute-start | bytes 393224 | tf_op jit(solution)/shard_map/ppermute | solution.py:295
  55.8 2.7 %collective-permute-start.27 = (bf16[264,256]{1,0:T(8,128)(2,1)S(1)}, bf16[264,256]{1,0:T(8,128)(2,1)S(1)}, u32[]{:S(2)}, u32[]{:S(2)}) collective-permute-start(bf16[264,256]{1,0:T(8,128)(2,1)S(1)} %collective-permute-done.23.refs_3_), channel_id=1, source_target_pairs={{0,4},{4,0},{8,12},{12,8},{16,20},{20,16},{24,28},{28,24},{1,5},{5... | collective-permute-start | bytes 405512 | tf_op jit(solution)/shard_map/ppermute | solution.py:295
  58.8 1.8 %collective-permute-start.16 = (bf16[256,256]{1,0:T(8,128)(2,1)S(1)}, bf16[256,256]{1,0:T(8,128)(2,1)S(1)}, u32[]{:S(2)}, u32[]{:S(2)}) collective-permute-start(bf16[256,256]{1,0:T(8,128)(2,1)S(1)} %collective-permute-done.14.refs_4_), channel_id=1, source_target_pairs={{0,8},{4,12},{8,0},{12,4},{16,24},{20,28},{24,16},{28,20},{1,9},{5... | collective-permute-start | bytes 393224 | tf_op jit(solution)/shard_map/ppermute | solution.py:295
  60.7 1.9 %collective-permute-start.22 = (bf16[264,256]{1,0:T(8,128)(2,1)S(1)}, bf16[264,256]{1,0:T(8,128)(2,1)S(1)}, u32[]{:S(2)}, u32[]{:S(2)}) collective-permute-start(bf16[264,256]{1,0:T(8,128)(2,1)S(1)} %collective-permute-done.21.refs_2_), channel_id=1, source_target_pairs={{0,4},{4,0},{8,12},{12,8},{16,20},{20,16},{24,28},{28,24},{1,5},{5... | collective-permute-start | bytes 405512 | tf_op jit(solution)/shard_map/ppermute | solution.py:295
  65.6 2.0 %collective-permute-done.17.refs_7_ = bf16[256,256]{1,0:T(8,128)(2,1)S(1)} collective-permute-done((bf16[256,256]{1,0:T(8,128)(2,1)S(1)}, bf16[256,256]{1,0:T(8,128)(2,1)S(1)}, u32[]{:S(2)}, u32[]{:S(2)}) %collective-permute-start.17) | collective-permute-done | bytes 131104 | tf_op jit(solution)/shard_map/ppermute | solution.py:295
  67.6 1.0 %unpack.3 = (bf16[1024,256]{1,0:T(8,128)(2,1)}, bf16[1024,256]{1,0:T(8,128)(2,1)}) custom-call(bf16[256,256]{1,0:T(8,128)(2,1)S(1)} %get-tuple-element.43.refs_0_, bf16[256,256]{1,0:T(8,128)(2,1)S(1)} %collective-permute-done.11.refs_1_, bf16[256,256]{1,0:T(8,128)(2,1)S(1)} %collective-permute-done.12.refs_2_, ...), custom_call_target="tpu_custom_call" | custom-call | tf_op jit(solution)/shard_map/unpack/pallas_call | solution.py:204
  68.6 1.3 %unpack.5 = (bf16[1024,256]{1,0:T(8,128)(2,1)}, bf16[256,1024]{1,0:T(8,128)(2,1)}, bf16[8,128]{1,0:T(8,128)(2,1)}, bf16[8,128]{1,0:T(8,128)(2,1)}) custom-call(bf16[264,256]{1,0:T(8,128)(2,1)S(1)} %collective-permute-done.22.refs_0_, bf16[264,256]{1,0:T(8,128)(2,1)S(1)} %collective-permute-done.25.refs_1_, ...), custom_call_target="tpu_custom_call", output_to_operand_aliasing={{0}: (3, {}), {1}: (4, {})} | custom-call | tf_op jit(solution)/shard_map/unpack/pallas_call | solution.py:204
  (77 shorter events, 9.1 us)
Async XLA Ops:
  2.2 33.2 %collective-permute-start.1 = (f16[272,256]{1,0:T(8,128)(2,1)S(1)}, f16[272,256]{1,0:T(8,128)(2,1)S(1)}, u32[]{:S(2)}, u32[]{:S(2)}) collective-permute-start(f16[272,256]{1,0:T(8,128)(2,1)S(1)} %get-tuple-element.64), channel_id=1, source_target_pairs={{0,4},{4,0},{8,12},{12,8},{16,20},{20,16},{24,28},{28,24},{1,5},{5... | collective-permute-start | bytes 417800 | tf_op jit(solution)/shard_map/ppermute | solution.py:295
  5.2 12.2 %collective-permute-start.5 = (f16[272,256]{1,0:T(8,128)(2,1)S(1)}, f16[272,256]{1,0:T(8,128)(2,1)S(1)}, u32[]{:S(2)}, u32[]{:S(2)}) collective-permute-start(f16[272,256]{1,0:T(8,128)(2,1)S(1)} %get-tuple-element.65), channel_id=1, source_target_pairs={{0,8},{4,12},{8,0},{12,4},{16,24},{20,28},{24,16},{28,20},{1,9},{5... | collective-permute-start | bytes 417800 | tf_op jit(solution)/shard_map/ppermute | solution.py:295
  6.9 12.3 %collective-permute-start.4 = (f16[256,256]{1,0:T(8,128)(2,1)S(1)}, f16[256,256]{1,0:T(8,128)(2,1)S(1)}, u32[]{:S(2)}, u32[]{:S(2)}) collective-permute-start(f16[256,256]{1,0:T(8,128)(2,1)S(1)} %get-tuple-element.66), channel_id=1, source_target_pairs={{0,4},{4,0},{8,12},{12,8},{16,20},{20,16},{24,28},{28,24},{1,5},{5... | collective-permute-start | bytes 393224 | tf_op jit(solution)/shard_map/ppermute | solution.py:295
  7.5 8.4 %collective-permute-start.6 = (f16[256,256]{1,0:T(8,128)(2,1)S(1)}, f16[256,256]{1,0:T(8,128)(2,1)S(1)}, u32[]{:S(2)}, u32[]{:S(2)}) collective-permute-start(f16[256,256]{1,0:T(8,128)(2,1)S(1)} %get-tuple-element.67), channel_id=1, source_target_pairs={{0,4},{4,0},{8,12},{12,8},{16,20},{20,16},{24,28},{28,24},{1,5},{5... | collective-permute-start | bytes 393224 | tf_op jit(solution)/shard_map/ppermute | solution.py:295
  9.0 16.2 %collective-permute-start.3 = (f16[256,256]{1,0:T(8,128)(2,1)S(1)}, f16[256,256]{1,0:T(8,128)(2,1)S(1)}, u32[]{:S(2)}, u32[]{:S(2)}) collective-permute-start(f16[256,256]{1,0:T(8,128)(2,1)S(1)} %get-tuple-element.68), channel_id=1, source_target_pairs={{0,4},{4,0},{8,12},{12,8},{16,20},{20,16},{24,28},{28,24},{1,5},{5... | collective-permute-start | bytes 393224 | tf_op jit(solution)/shard_map/ppermute | solution.py:295
  15.9 19.6 %collective-permute-start = (f16[256,256]{1,0:T(8,128)(2,1)S(1)}, f16[256,256]{1,0:T(8,128)(2,1)S(1)}, u32[]{:S(2)}, u32[]{:S(2)}) collective-permute-start(f16[256,256]{1,0:T(8,128)(2,1)S(1)} %fusion.40), channel_id=1, source_target_pairs={{0,4},{4,0},{8,12},{12,8},{16,20},{20,16},{24,28},{28,24},{1,5},{5... | collective-permute-start | bytes 393224 | tf_op jit(solution)/shard_map/ppermute | solution.py:295
  17.5 6.0 %collective-permute-start.7 = (f16[256,256]{1,0:T(8,128)(2,1)S(1)}, f16[256,256]{1,0:T(8,128)(2,1)S(1)}, u32[]{:S(2)}, u32[]{:S(2)}) collective-permute-start(f16[256,256]{1,0:T(8,128)(2,1)S(1)} %fusion.21), channel_id=1, source_target_pairs={{0,8},{4,12},{8,0},{12,4},{16,24},{20,28},{24,16},{28,20},{1,9},{5... | collective-permute-start | bytes 393224 | tf_op jit(solution)/shard_map/ppermute | solution.py:295
  19.2 29.3 %collective-permute-start.20 = (f16[272,256]{1,0:T(8,128)(2,1)S(1)}, f16[272,256]{1,0:T(8,128)(2,1)S(1)}, u32[]{:S(2)}, u32[]{:S(2)}) collective-permute-start(f16[272,256]{1,0:T(8,128)(2,1)S(1)} %get-tuple-element.62), channel_id=1, source_target_pairs={{0,4},{4,0},{8,12},{12,8},{16,20},{20,16},{24,28},{28,24},{1,5},{5... | collective-permute-start | bytes 417800 | tf_op jit(solution)/shard_map/ppermute | solution.py:295
  23.5 7.5 %collective-permute-start.2 = (f16[272,256]{1,0:T(8,128)(2,1)S(1)}, f16[272,256]{1,0:T(8,128)(2,1)S(1)}, u32[]{:S(2)}, u32[]{:S(2)}) collective-permute-start(f16[272,256]{1,0:T(8,128)(2,1)S(1)} %get-tuple-element.63), channel_id=1, source_target_pairs={{0,8},{4,12},{8,0},{12,4},{16,24},{20,28},{24,16},{28,20},{1,9},{5... | collective-permute-start | bytes 417800 | tf_op jit(solution)/shard_map/ppermute | solution.py:295
  25.1 6.3 %collective-permute-start.8 = (f16[272,256]{1,0:T(8,128)(2,1)S(1)}, f16[272,256]{1,0:T(8,128)(2,1)S(1)}, u32[]{:S(2)}, u32[]{:S(2)}) collective-permute-start(f16[272,256]{1,0:T(8,128)(2,1)S(1)} %fusion.8), channel_id=1, source_target_pairs={{0,4},{4,0},{8,12},{12,8},{16,20},{20,16},{24,28},{28,24},{1,5},{5... | collective-permute-start | bytes 417800 | tf_op jit(solution)/shard_map/ppermute | solution.py:295
  31.0 9.2 %collective-permute-start.10 = (f16[256,256]{1,0:T(8,128)(2,1)S(1)}, f16[256,256]{1,0:T(8,128)(2,1)S(1)}, u32[]{:S(2)}, u32[]{:S(2)}) collective-permute-start(f16[256,256]{1,0:T(8,128)(2,1)S(1)} %fusion.30), channel_id=1, source_target_pairs={{0,8},{4,12},{8,0},{12,4},{16,24},{20,28},{24,16},{28,20},{1,9},{5... | collective-permute-start | bytes 393224 | tf_op jit(solution)/shard_map/ppermute | solution.py:295
  31.4 11.7 %collective-permute-start.9 = (f16[256,256]{1,0:T(8,128)(2,1)S(1)}, f16[256,256]{1,0:T(8,128)(2,1)S(1)}, u32[]{:S(2)}, u32[]{:S(2)}) collective-permute-start(f16[256,256]{1,0:T(8,128)(2,1)S(1)} %fusion.26), channel_id=1, source_target_pairs={{0,16},{4,20},{8,24},{12,28},{16,0},{20,4},{24,8},{28,12},{1,17},{... | collective-permute-start | bytes 393224 | tf_op jit(solution)/shard_map/ppermute | solution.py:295
  35.4 13.0 %collective-permute-start.18 = (f16[272,256]{1,0:T(8,128)(2,1)S(1)}, f16[272,256]{1,0:T(8,128)(2,1)S(1)}, u32[]{:S(2)}, u32[]{:S(2)}) collective-permute-start(f16[272,256]{1,0:T(8,128)(2,1)S(1)} %fusion.13), channel_id=1, source_target_pairs={{0,16},{4,20},{8,24},{12,28},{16,0},{20,4},{24,8},{28,12},{1,17},{... | collective-permute-start | bytes 417800 | tf_op jit(solution)/shard_map/ppermute | solution.py:295
  35.5 12.9 %collective-permute-start.19 = (f16[272,256]{1,0:T(8,128)(2,1)S(1)}, f16[272,256]{1,0:T(8,128)(2,1)S(1)}, u32[]{:S(2)}, u32[]{:S(2)}) collective-permute-start(f16[272,256]{1,0:T(8,128)(2,1)S(1)} %fusion.17), channel_id=1, source_target_pairs={{0,8},{4,12},{8,0},{12,4},{16,24},{20,28},{24,16},{28,20},{1,9},{5... | collective-permute-start | bytes 417800 | tf_op jit(solution)/shard_map/ppermute | solution.py:295
  44.0 7.4 %collective-permute-start.14 = (bf16[256,256]{1,0:T(8,128)(2,1)S(1)}, bf16[256,256]{1,0:T(8,128)(2,1)S(1)}, u32[]{:S(2)}, u32[]{:S(2)}) collective-permute-start(bf16[256,256]{1,0:T(8,128)(2,1)S(1)} %get-tuple-element.43.refs_0_), channel_id=1, source_target_pairs={{0,16},{4,20},{8,24},{12,28},{16,0},{20,4},{24,8},{28,12},{1,17},{... | collective-permute-start | bytes 393224 | tf_op jit(solution)/shard_map/ppermute | solution.py:295
  44.0 10.4 %collective-permute-start.12 = (bf16[256,256]{1,0:T(8,128)(2,1)S(1)}, bf16[256,256]{1,0:T(8,128)(2,1)S(1)}, u32[]{:S(2)}, u32[]{:S(2)}) collective-permute-start(bf16[256,256]{1,0:T(8,128)(2,1)S(1)} %get-tuple-element.43.refs_0_), channel_id=1, source_target_pairs={{0,8},{4,12},{8,0},{12,4},{16,24},{20,28},{24,16},{28,20},{1,9},{5... | collective-permute-start | bytes 393224 | tf_op jit(solution)/shard_map/ppermute | solution.py:295
  48.4 10.1 %collective-permute-start.11 = (bf16[256,256]{1,0:T(8,128)(2,1)S(1)}, bf16[256,256]{1,0:T(8,128)(2,1)S(1)}, u32[]{:S(2)}, u32[]{:S(2)}) collective-permute-start(bf16[256,256]{1,0:T(8,128)(2,1)S(1)} %get-tuple-element.43.refs_0_), channel_id=1, source_target_pairs={{0,4},{4,0},{8,12},{12,8},{16,20},{20,16},{24,28},{28,24},{1,5},{5... | collective-permute-start | bytes 393224 | tf_op jit(solution)/shard_map/ppermute | solution.py:295
  49.3 6.5 %collective-permute-start.23 = (bf16[264,256]{1,0:T(8,128)(2,1)S(1)}, bf16[264,256]{1,0:T(8,128)(2,1)S(1)}, u32[]{:S(2)}, u32[]{:S(2)}) collective-permute-start(bf16[264,256]{1,0:T(8,128)(2,1)S(1)} %get-tuple-element.47.refs_0_), channel_id=1, source_target_pairs={{0,16},{4,20},{8,24},{12,28},{16,0},{20,4},{24,8},{28,12},{1,17},{... | collective-permute-start | bytes 405512 | tf_op jit(solution)/shard_map/ppermute | solution.py:295
  49.3 9.5 %collective-permute-start.26 = (bf16[264,256]{1,0:T(8,128)(2,1)S(1)}, bf16[264,256]{1,0:T(8,128)(2,1)S(1)}, u32[]{:S(2)}, u32[]{:S(2)}) collective-permute-start(bf16[264,256]{1,0:T(8,128)(2,1)S(1)} %get-tuple-element.47.refs_0_), channel_id=1, source_target_pairs={{0,4},{4,0},{8,12},{12,8},{16,20},{20,16},{24,28},{28,24},{1,5},{5... | collective-permute-start | bytes 405512 | tf_op jit(solution)/shard_map/ppermute | solution.py:295
  51.4 9.2 %collective-permute-start.21 = (bf16[264,256]{1,0:T(8,128)(2,1)S(1)}, bf16[264,256]{1,0:T(8,128)(2,1)S(1)}, u32[]{:S(2)}, u32[]{:S(2)}) collective-permute-start(bf16[264,256]{1,0:T(8,128)(2,1)S(1)} %get-tuple-element.47.refs_0_), channel_id=1, source_target_pairs={{0,8},{4,12},{8,0},{12,4},{16,24},{20,28},{24,16},{28,20},{1,9},{5... | collective-permute-start | bytes 405512 | tf_op jit(solution)/shard_map/ppermute | solution.py:295
  54.4 6.3 %collective-permute-start.15 = (bf16[256,256]{1,0:T(8,128)(2,1)S(1)}, bf16[256,256]{1,0:T(8,128)(2,1)S(1)}, u32[]{:S(2)}, u32[]{:S(2)}) collective-permute-start(bf16[256,256]{1,0:T(8,128)(2,1)S(1)} %collective-permute-done.14.refs_4_), channel_id=1, source_target_pairs={{0,4},{4,0},{8,12},{12,8},{16,20},{20,16},{24,28},{28,24},{1,5},{5... | collective-permute-start | bytes 393224 | tf_op jit(solution)/shard_map/ppermute | solution.py:295
  55.8 6.8 %collective-permute-start.27 = (bf16[264,256]{1,0:T(8,128)(2,1)S(1)}, bf16[264,256]{1,0:T(8,128)(2,1)S(1)}, u32[]{:S(2)}, u32[]{:S(2)}) collective-permute-start(bf16[264,256]{1,0:T(8,128)(2,1)S(1)} %collective-permute-done.23.refs_3_), channel_id=1, source_target_pairs={{0,4},{4,0},{8,12},{12,8},{16,20},{20,16},{24,28},{28,24},{1,5},{5... | collective-permute-start | bytes 405512 | tf_op jit(solution)/shard_map/ppermute | solution.py:295
  58.8 6.1 %collective-permute-start.16 = (bf16[256,256]{1,0:T(8,128)(2,1)S(1)}, bf16[256,256]{1,0:T(8,128)(2,1)S(1)}, u32[]{:S(2)}, u32[]{:S(2)}) collective-permute-start(bf16[256,256]{1,0:T(8,128)(2,1)S(1)} %collective-permute-done.14.refs_4_), channel_id=1, source_target_pairs={{0,8},{4,12},{8,0},{12,4},{16,24},{20,28},{24,16},{28,20},{1,9},{5... | collective-permute-start | bytes 393224 | tf_op jit(solution)/shard_map/ppermute | solution.py:295
  60.7 7.8 %collective-permute-start.22 = (bf16[264,256]{1,0:T(8,128)(2,1)S(1)}, bf16[264,256]{1,0:T(8,128)(2,1)S(1)}, u32[]{:S(2)}, u32[]{:S(2)}) collective-permute-start(bf16[264,256]{1,0:T(8,128)(2,1)S(1)} %collective-permute-done.21.refs_2_), channel_id=1, source_target_pairs={{0,4},{4,0},{8,12},{12,8},{16,20},{20,16},{24,28},{28,24},{1,5},{5... | collective-permute-start | bytes 405512 | tf_op jit(solution)/shard_map/ppermute | solution.py:295
  (10 other events, 179.2 us)
